TPU v7x, 32 devices: a 4x4x1 block of a 4x4x8 slice. The times are simulated.
32 devices in a mesh: dp: 1 (over z), col: 4 (over y), row: 8 (over x, core).
Axes of the slice: x: 4, y: 4, z: 1, core: 2. Of those that a mesh axis runs over, the one named last changes fastest.
The devices are a block of a 4x4x8 slice.
Arguments:
- hidden: bfloat16 [64, 4096], P('dp', 'row')
- cache_len: int32 [64], P('dp')
- k_cache: bfloat16 [2, 64, 32, 256, 128], P(None, 'dp', ('col', 'row'))
- v_cache: bfloat16 [2, 64, 32, 256, 128], P(None, 'dp', ('col', 'row'))
- ln1_g: bfloat16 [2, 4096], P(None, 'row')
- ln1_b: bfloat16 [2, 4096], P(None, 'row')
- w_q: bfloat16 [2, 4096, 4096], P(None, 'row', 'col')
- b_q: bfloat16 [2, 4096], P(None, 'col')
- w_k: bfloat16 [2, 4096, 4096], P(None, 'row', 'col')
- b_k: bfloat16 [2, 4096], P(None, 'col')
- w_v: bfloat16 [2, 4096, 4096], P(None, 'row', 'col')
- b_v: bfloat16 [2, 4096], P(None, 'col')
- w_o: bfloat16 [2, 4096, 4096], P(None, 'col', 'row')
- b_o: bfloat16 [2, 4096], P(None, 'row')
- ln2_g: bfloat16 [2, 4096], P(None, 'row')
- ln2_b: bfloat16 [2, 4096], P(None, 'row')
- w_fc1: bfloat16 [2, 4096, 16384], P(None, 'row', 'col')
- b_fc1: bfloat16 [2, 16384], P(None, 'col')
- w_fc2: bfloat16 [2, 16384, 4096], P(None, 'col', 'row')
- b_fc2: bfloat16 [2, 4096], P(None, 'row')
Outputs:
- output 1: bfloat16 [64, 4096], P('dp', 'row')
- output 2: bfloat16 [2, 64, 32, 128], P(None, 'dp', ('col', 'row'))
- output 3: bfloat16 [2, 64, 32, 128], P(None, 'dp', ('col', 'row'))
All inputs are finite; a program needn't handle non-finite values.
Results may differ from a plain program's by a relative error of at most 0.02.
Values are sent between devices in bfloat16 or wider.
A program may use at most 768 MiB of HBM per device.

v0:
```python
import jax
import jax.numpy as jnp
from jax import lax
from jax.sharding import PartitionSpec as P

EPS_LN = 1e-5


def attention(q_heads, k_fresh, v_fresh, k_layer, v_layer, lengths):
    scores = jnp.einsum("bhd,bhsd->bhs", q_heads, k_layer, preferred_element_type=jnp.float32)
    positions = jnp.arange(k_layer.shape[2])
    scores = jnp.where(positions[None, None, :] < lengths[:, None, None], scores, -jnp.inf)
    score_new = jnp.einsum("bhd,bhd->bh", q_heads, k_fresh, preferred_element_type=jnp.float32)
    peak = jnp.maximum(jnp.max(scores, axis=-1), score_new)
    exp_cache = jnp.exp(scores - peak[:, :, None])
    exp_new = jnp.exp(score_new - peak)
    total_mass = jnp.sum(exp_cache, axis=-1) + exp_new
    prob_cache = (exp_cache / total_mass[:, :, None]).astype(jnp.bfloat16)
    prob_new = (exp_new / total_mass).astype(jnp.bfloat16)
    mixed = jnp.einsum("bhs,bhsd->bhd", prob_cache, v_layer, preferred_element_type=jnp.float32)
    mixed = mixed + prob_new.astype(jnp.float32)[:, :, None] * v_fresh.astype(jnp.float32)
    return mixed.astype(jnp.bfloat16)


def solution(mesh):
    n_row = mesh.shape["row"]
    act_spec = P("dp", "row")
    cache_spec = P(None, "dp", ("col", "row"), None, None)
    fresh_spec = P(None, "dp", ("col", "row"), None)
    in_weight = P(None, "row", "col")
    out_weight = P(None, "col", "row")
    col_vec = P(None, "col")
    row_vec = P(None, "row")
    in_specs = (act_spec, P("dp"), cache_spec, cache_spec, row_vec, row_vec,
                in_weight, col_vec, in_weight, col_vec, in_weight, col_vec,
                out_weight, row_vec, row_vec, row_vec, in_weight, col_vec, out_weight, row_vec)

    def layer_norm(state, gain, shift):
        state_f32 = state.astype(jnp.float32)
        stats = jnp.stack([jnp.sum(state_f32, axis=-1), jnp.sum(state_f32 * state_f32, axis=-1)], axis=-1)
        stats = lax.psum(stats, "row")
        width = state.shape[-1] * n_row
        mean_val = stats[:, 0:1] / width
        variance = stats[:, 1:2] / width - mean_val * mean_val
        normed = (state_f32 - mean_val) * lax.rsqrt(variance + EPS_LN) * gain.astype(jnp.float32) + shift.astype(jnp.float32)
        return normed.astype(jnp.bfloat16)

    def head_projection(normed, weight, bias, scale):
        partial = jnp.dot(normed, weight, preferred_element_type=jnp.float32).astype(jnp.bfloat16)
        summed = lax.psum_scatter(partial, "row", scatter_dimension=1, tiled=True)
        width = summed.shape[1]
        bias_own = lax.dynamic_slice_in_dim(bias, lax.axis_index("row") * width, width)
        return ((summed.astype(jnp.float32) + bias_own.astype(jnp.float32)) * scale).astype(jnp.bfloat16)

    def local_step(hidden, cache_len, k_cache, v_cache, ln1_g, ln1_b, w_q, b_q, w_k, b_k, w_v, b_v,
                   w_o, b_o, ln2_g, ln2_b, w_fc1, b_fc1, w_fc2, b_fc2):
        batch_rows = hidden.shape[0]
        heads_dev = k_cache.shape[2]
        head_dim = k_cache.shape[4]
        scale = head_dim ** -0.5
        state = hidden
        k_rows = []
        v_rows = []
        for layer in range(w_q.shape[0]):
            normed = layer_norm(state, ln1_g[layer], ln1_b[layer])
            q_heads = head_projection(normed, w_q[layer], b_q[layer], scale).reshape(batch_rows, heads_dev, head_dim)
            k_fresh = head_projection(normed, w_k[layer], b_k[layer], 1.0).reshape(batch_rows, heads_dev, head_dim)
            v_fresh = head_projection(normed, w_v[layer], b_v[layer], 1.0).reshape(batch_rows, heads_dev, head_dim)
            attended = attention(q_heads, k_fresh, v_fresh, k_cache[layer], v_cache[layer], cache_len)
            gathered = lax.all_gather(attended.reshape(batch_rows, heads_dev * head_dim), "row", axis=1, tiled=True)
            proj_part = jnp.dot(gathered, w_o[layer], preferred_element_type=jnp.float32).astype(jnp.bfloat16)
            projected = lax.psum(proj_part, "col")
            state_mid = (state.astype(jnp.float32) + (projected.astype(jnp.float32) + b_o[layer].astype(jnp.float32))).astype(jnp.bfloat16)
            normed_two = layer_norm(state_mid, ln2_g[layer], ln2_b[layer])
            inner_part = jnp.dot(normed_two, w_fc1[layer], preferred_element_type=jnp.float32).astype(jnp.bfloat16)
            inner_sum = lax.psum(inner_part, "row")
            inner = jnp.maximum((inner_sum.astype(jnp.float32) + b_fc1[layer].astype(jnp.float32)).astype(jnp.bfloat16), 0)
            out_part = jnp.dot(inner, w_fc2[layer], preferred_element_type=jnp.float32).astype(jnp.bfloat16)
            out_sum = lax.psum(out_part, "col")
            state = (state_mid.astype(jnp.float32) + (out_sum.astype(jnp.float32) + b_fc2[layer].astype(jnp.float32))).astype(jnp.bfloat16)
            k_rows.append(k_fresh)
            v_rows.append(v_fresh)
        return state, jnp.stack(k_rows), jnp.stack(v_rows)

    return jax.shard_map(local_step, mesh=mesh, in_specs=in_specs,
                         out_specs=(act_spec, fresh_spec, fresh_spec), check_vma=False)
```

profile of v0, /device:TPU:97, one launch (start us, length us, event | category | flops | bytes accessed | tf_op | source)
XLA Modules:
  0.0 568.5 jit_solution(18045851487847616652)
XLA Ops:
  7.3 1.1 convert_reduce_fusion.3
  8.4 13.9 %psum.70 = f32[64,2]{0,1:T(2,128)S(1)} all-reduce(f32[64,2]{0,1:T(2,128)S(1)} %pad_maximum_fusion.2), channel_id=1, replica_groups=mesh['dp'=1,'col'=4,'row'=8] {'row'}, use_global_device_ids=true, to_apply=%region_2.0 | all-reduce | flops 128 | bytes 1024 | tf_op jit(solution)/shard_map/psum | solution.py:41
  23.8 1.6 convolution_convert_fusion.6
  26.4 1.6 convolution_convert_fusion.7
  30.5 24.0 %reduce-scatter.21.cloned.1.call-done = bf16[128,64]{1,0:T(8,128)(2,1)} async-done(((bf16[1024,64]{1,0:T(8,128)(2,1)}), bf16[128,64]{1,0:T(8,128)(2,1)}) %reduce-scatter.21.cloned.1.call-update) | async-done | bytes 16400
  55.4 28.6 %reduce-scatter.19.cloned.1.call-done = bf16[128,64]{1,0:T(8,128)(2,1)} async-done(((bf16[1024,64]{1,0:T(8,128)(2,1)}), bf16[128,64]{1,0:T(8,128)(2,1)}) %reduce-scatter.19.cloned.1.call-update) | async-done | bytes 16400
  85.0 3.5 fusion.12
  89.1 24.5 %reduce-scatter.23.cloned.1.call-done = bf16[128,64]{1,0:T(8,128)(2,1)} async-done(((bf16[1024,64]{1,0:T(8,128)(2,1)}), bf16[128,64]{1,0:T(8,128)(2,1)}) %reduce-scatter.23.cloned.1.call-update) | async-done | bytes 16400
  114.4 2.8 fusion.10
  117.3 18.9 %all_gather.6 = bf16[64,1024]{1,0:T(8,128)(2,1)S(1)} all-gather(bf16[64,128]{1,0:T(8,128)(2,1)S(1)} %get-tuple-element.15), channel_id=1, replica_groups=mesh['dp'=1,'col'=4,'row'=8] {'row'}, dimensions={1}, use_global_device_ids=true | all-gather | bytes 147456 | tf_op jit(solution)/shard_map/all_gather | solution.py:70
  137.3 40.2 %all-reduce.7.cloned.1.call-done = bf16[64,512]{1,0:T(8,128)(2,1)} async-done(((bf16[64,512]{1,0:T(8,128)(2,1)}), bf16[64,512]{1,0:T(8,128)(2,1)}) %all-reduce.7.cloned.1.call-update) | async-done | bytes 65552 | tf_op jit(solution)/shard_map/psum | solution.py:72
  178.5 14.5 %psum.72 = f32[64,2]{0,1:T(2,128)S(1)} all-reduce(f32[64,2]{0,1:T(2,128)S(1)} %pad_maximum_fusion.3), channel_id=1, replica_groups=mesh['dp'=1,'col'=4,'row'=8] {'row'}, use_global_device_ids=true, to_apply=%region_11.12 | all-reduce | flops 128 | bytes 1024 | tf_op jit(solution)/shard_map/psum | solution.py:41
  193.0 3.9 convolution_convert_fusion.1
  197.1 52.0 %all-reduce.9.cloned.1.call-done = bf16[64,4096]{1,0:T(8,128)(2,1)} async-done(((bf16[64,4096]{1,0:T(8,128)(2,1)}), bf16[64,4096]{1,0:T(8,128)(2,1)}) %all-reduce.9.cloned.1.call-update) | async-done | bytes 524304 | tf_op jit(solution)/shard_map/psum | solution.py:76
  249.1 3.7 fusion.22
  253.0 35.4 %all-reduce.11.cloned.1.call-done = bf16[64,512]{1,0:T(8,128)(2,1)} async-done(((bf16[64,512]{1,0:T(8,128)(2,1)}), bf16[64,512]{1,0:T(8,128)(2,1)}) %all-reduce.11.cloned.1.call-update) | async-done | bytes 65552 | tf_op jit(solution)/shard_map/psum | solution.py:79
  289.4 14.5 %psum.75 = f32[64,2]{0,1:T(2,128)S(1)} all-reduce(f32[64,2]{0,1:T(2,128)S(1)} %pad_maximum_fusion.4), channel_id=1, replica_groups=mesh['dp'=1,'col'=4,'row'=8] {'row'}, use_global_device_ids=true, to_apply=%region_16.17 | all-reduce | flops 128 | bytes 1024 | tf_op jit(solution)/shard_map/psum | solution.py:41
  305.3 1.6 convolution_convert_fusion.4
  307.8 1.6 convolution_convert_fusion.2
  310.4 18.8 %reduce-scatter.27.cloned.1.call-done = bf16[128,64]{1,0:T(8,128)(2,1)} async-done(((bf16[1024,64]{1,0:T(8,128)(2,1)}), bf16[128,64]{1,0:T(8,128)(2,1)}) %reduce-scatter.27.cloned.1.call-update) | async-done | bytes 16400
  330.0 28.6 %reduce-scatter.25.cloned.1.call-done = bf16[128,64]{1,0:T(8,128)(2,1)} async-done(((bf16[1024,64]{1,0:T(8,128)(2,1)}), bf16[128,64]{1,0:T(8,128)(2,1)}) %reduce-scatter.25.cloned.1.call-update) | async-done | bytes 16400
  359.6 3.5 fusion.5
  363.7 2.8 fusion.3
  366.5 21.6 %reduce-scatter.29.cloned.1.call-done = bf16[128,64]{1,0:T(8,128)(2,1)} async-done(((bf16[1024,64]{1,0:T(8,128)(2,1)}), bf16[128,64]{1,0:T(8,128)(2,1)}) %reduce-scatter.29.cloned.1.call-update) | async-done | bytes 16400
  389.1 18.9 %all_gather.7 = bf16[64,1024]{1,0:T(8,128)(2,1)S(1)} all-gather(bf16[64,128]{1,0:T(8,128)(2,1)S(1)} %get-tuple-element.17), channel_id=1, replica_groups=mesh['dp'=1,'col'=4,'row'=8] {'row'}, dimensions={1}, use_global_device_ids=true | all-gather | bytes 147456 | tf_op jit(solution)/shard_map/all_gather | solution.py:70
  409.1 40.2 %all-reduce.13.cloned.1.call-done = bf16[64,512]{1,0:T(8,128)(2,1)} async-done(((bf16[64,512]{1,0:T(8,128)(2,1)}), bf16[64,512]{1,0:T(8,128)(2,1)}) %all-reduce.13.cloned.1.call-update) | async-done | bytes 65552 | tf_op jit(solution)/shard_map/psum | solution.py:72
  450.3 14.5 %psum.77 = f32[64,2]{0,1:T(2,128)S(1)} all-reduce(f32[64,2]{0,1:T(2,128)S(1)} %pad_maximum_fusion.5), channel_id=1, replica_groups=mesh['dp'=1,'col'=4,'row'=8] {'row'}, use_global_device_ids=true, to_apply=%region_25.26 | all-reduce | flops 128 | bytes 1024 | tf_op jit(solution)/shard_map/psum | solution.py:41
  464.8 3.9 convolution_convert_fusion
  469.4 51.4 %all-reduce.15.cloned.1.call-done = bf16[64,4096]{1,0:T(8,128)(2,1)} async-done(((bf16[64,4096]{1,0:T(8,128)(2,1)}), bf16[64,4096]{1,0:T(8,128)(2,1)}) %all-reduce.15.cloned.1.call-update) | async-done | bytes 524304 | tf_op jit(solution)/shard_map/psum | solution.py:76
  520.9 3.7 fusion.25
  525.3 34.9 %all-reduce.17.cloned.1.call-done = bf16[64,512]{1,0:T(8,128)(2,1)} async-done(((bf16[64,512]{1,0:T(8,128)(2,1)}), bf16[64,512]{1,0:T(8,128)(2,1)}) %all-reduce.17.cloned.1.call-update) | async-done | bytes 65552 | tf_op jit(solution)/shard_map/psum | solution.py:79
  560.2 1.5 fusion.75
  (109 shorter events, 21.4 us)
Async XLA Ops:
  7.2 21.8 %copy-start = (bf16[64,512]{1,0:T(8,128)(2,1)S(1)}, bf16[64,512]{1,0:T(8,128)(2,1)}, u32[]{:S(2)}) copy-start(bf16[64,512]{1,0:T(8,128)(2,1)} %param.20) | copy-start | bytes 196612
  7.2 21.8 %copy-start.11 = (bf16[2,512,1024]{2,1,0:T(8,128)(2,1)S(1)}, bf16[2,512,1024]{2,1,0:T(8,128)(2,1)}, u32[]{:S(2)}) copy-start(bf16[2,512,1024]{2,1,0:T(8,128)(2,1)} %param.30) | copy-start | bytes 6291460
  7.2 23.2 %copy-start.6 = (bf16[2,512]{1,0:T(2,128)(2,1)S(1)}, bf16[2,512]{1,0:T(2,128)(2,1)}, u32[]{:S(2)}) copy-start(bf16[2,512]{1,0:T(2,128)(2,1)} %param.33) | copy-start | bytes 6148
  7.2 23.2 %copy-start.7 = (bf16[2,512]{1,0:T(2,128)(2,1)S(1)}, bf16[2,512]{1,0:T(2,128)(2,1)}, u32[]{:S(2)}) copy-start(bf16[2,512]{1,0:T(2,128)(2,1)} %param.34) | copy-start | bytes 6148
  7.2 23.2 %copy-start.3 = (bf16[2,1024]{1,0:T(2,128)(2,1)S(1)}, bf16[2,1024]{1,0:T(2,128)(2,1)}, u32[]{:S(2)}) copy-start(bf16[2,1024]{1,0:T(2,128)(2,1)} %param.27) | copy-start | bytes 12292
  7.2 23.2 %copy-start.4 = (bf16[2,1024]{1,0:T(2,128)(2,1)S(1)}, bf16[2,1024]{1,0:T(2,128)(2,1)}, u32[]{:S(2)}) copy-start(bf16[2,1024]{1,0:T(2,128)(2,1)} %param.29) | copy-start | bytes 12292
  7.2 23.2 %copy-start.5 = (bf16[2,1024]{1,0:T(2,128)(2,1)S(1)}, bf16[2,1024]{1,0:T(2,128)(2,1)}, u32[]{:S(2)}) copy-start(bf16[2,1024]{1,0:T(2,128)(2,1)} %param.31) | copy-start | bytes 12292
  7.3 47.3 %reduce-scatter.21.cloned.1.call-start = ((), (), s32[]{:S(2)}) async-start(), calls=%async_computation.13 | async-start | bytes 294912
  26.3 62.2 %copy-start.2 = (s32[64]{0:T(128)S(1)}, s32[64]{0:T(128)}, u32[]{:S(2)}) copy-start(s32[64]{0:T(128)} %param.21) | copy-start | bytes 772
  26.4 57.7 %reduce-scatter.19.cloned.1.call-start = ((), (), s32[]{:S(2)}) async-start(), calls=%async_computation.12 | async-start | bytes 294912
  28.9 84.6 %reduce-scatter.23.cloned.1.call-start = ((), (), s32[]{:S(2)}) async-start(), calls=%async_computation.14 | async-start | bytes 294912
  30.3 147.2 %all-reduce.7.cloned.1.call-start = ((), (), s32[]{:S(2)}) async-start(), calls=%async_computation.6 | async-start | bytes 131072 | tf_op jit(solution)/shard_map/psum | solution.py:72
  85.0 51.2 %copy-start.12 = (bf16[2,1024,512]{2,1,0:T(8,128)(2,1)S(1)}, bf16[2,1024,512]{2,1,0:T(8,128)(2,1)}, u32[]{:S(2)}) copy-start(bf16[2,1024,512]{2,1,0:T(8,128)(2,1)} %param.32) | copy-start | bytes 6291460
  88.5 48.7 %copy-start.8 = (bf16[2,512]{1,0:T(2,128)(2,1)S(1)}, bf16[2,512]{1,0:T(2,128)(2,1)}, u32[]{:S(2)}) copy-start(bf16[2,512]{1,0:T(2,128)(2,1)} %param.35) | copy-start | bytes 6148
  117.2 79.8 %copy-start.1 = (bf16[2,4096]{1,0:T(2,128)(2,1)S(1)}, bf16[2,4096]{1,0:T(2,128)(2,1)}, u32[]{:S(2)}) copy-start(bf16[2,4096]{1,0:T(2,128)(2,1)} %param.37) | copy-start | bytes 49156
  137.2 111.9 %all-reduce.9.cloned.1.call-start = ((), (), s32[]{:S(2)}) async-start(), calls=%async_computation.7 | async-start | bytes 1048576 | tf_op jit(solution)/shard_map/psum | solution.py:76
  196.9 56.1 %copy-start.9 = (bf16[2,512]{1,0:T(2,128)(2,1)S(1)}, bf16[2,512]{1,0:T(2,128)(2,1)}, u32[]{:S(2)}) copy-start(bf16[2,512]{1,0:T(2,128)(2,1)} %param.39) | copy-start | bytes 6148
  196.9 107.0 %copy-start.10 = (bf16[2,512,1024]{2,1,0:T(8,128)(2,1)S(1)}, bf16[2,512,1024]{2,1,0:T(8,128)(2,1)}, u32[]{:S(2)}) copy-start(bf16[2,512,1024]{2,1,0:T(8,128)(2,1)} %param.28) | copy-start | bytes 6291460
  196.9 91.5 %all-reduce.11.cloned.1.call-start = ((), (), s32[]{:S(2)}) async-start(), calls=%async_computation.8 | async-start | bytes 131072 | tf_op jit(solution)/shard_map/psum | solution.py:79
  252.9 76.3 %reduce-scatter.27.cloned.1.call-start = ((), (), s32[]{:S(2)}) async-start(), calls=%async_computation.16 | async-start | bytes 294912
  305.2 53.5 %reduce-scatter.25.cloned.1.call-start = ((), (), s32[]{:S(2)}) async-start(), calls=%async_computation.15 | async-start | bytes 294912
  307.7 80.4 %reduce-scatter.29.cloned.1.call-start = ((), (), s32[]{:S(2)}) async-start(), calls=%async_computation.17 | async-start | bytes 294912
  310.3 139.0 %all-reduce.13.cloned.1.call-start = ((), (), s32[]{:S(2)}) async-start(), calls=%async_computation.9 | async-start | bytes 131072 | tf_op jit(solution)/shard_map/psum | solution.py:72
  359.6 48.4 %copy-start.13 = (bf16[2,1024,512]{2,1,0:T(8,128)(2,1)S(1)}, bf16[2,1024,512]{2,1,0:T(8,128)(2,1)}, u32[]{:S(2)}) copy-start(bf16[2,1024,512]{2,1,0:T(8,128)(2,1)} %param.32) | copy-start | bytes 6291460
  409.0 111.8 %all-reduce.15.cloned.1.call-start = ((), (), s32[]{:S(2)}) async-start(), calls=%async_computation.10 | async-start | bytes 1048576 | tf_op jit(solution)/shard_map/psum | solution.py:76
  468.7 91.5 %all-reduce.17.cloned.1.call-start = ((), (), s32[]{:S(2)}) async-start(), calls=%async_computation.11 | async-start | bytes 131072 | tf_op jit(solution)/shard_map/psum | solution.py:79
Sparse Core Ops, SparseCore 0:
  26.5 28.0 reduce-scatter.20
  56.8 27.1 reduce-scatter.18
  86.3 27.1 reduce-scatter.22
  137.3 40.1 all-reduce.6
  197.1 51.9 all-reduce.8
  253.0 35.3 all-reduce.10
  305.3 23.8 reduce-scatter.26
  331.5 27.1 reduce-scatter.24
  360.9 27.1 reduce-scatter.28
  409.1 40.0 all-reduce.12
  468.8 51.9 all-reduce.14
  524.8 35.3 all-reduce.16
where the time goes:
time: 571 us; the launch traced here: 569 us
  waiting for transfers between devices  401 us (70%)
  blocking collectives  95.2 us (17%)
  matrix products  36.9 us (6%)
  between operations  14.7 us (3%)
  local copies, waits for them, and re-layouts  10.1 us (2%)
  other arithmetic  9.87 us (2%)
    unnamed x18, waiting for transfers between devices  147 us
    psum x2, waiting for transfers between devices, local_step(): inner_sum = lax.psum(inner_part, 'row')  103 us
    psum x2, waiting for transfers between devices, local_step(): projected = lax.psum(proj_part, 'col')  80.4 us
    psum x2, waiting for transfers between devices, local_step(): out_sum = lax.psum(out_part, 'col')  70.4 us
    psum x4, blocking collectives, layer_norm(): stats = lax.psum(stats, 'row')  57.3 us
    all_gather x2, blocking collectives, local_step(): lax.all_gather(attended.reshape(batch_rows, heads_dev * head_dim), 'row',...  37.8 us
  transfers between devices with their start and end apart: 12, of which 12 were waited for; matrix products, arithmetic and copies ran while one was open for 4% of the time, Pallas kernels for 0%

commit v1 on v0

v1 whole, which is shorter than its diff:
```python
import functools

import jax
import jax.numpy as jnp
from jax import lax
from jax.experimental import pallas as pl
from jax.experimental.pallas import tpu as pltpu
from jax.sharding import PartitionSpec as P

EPS_LN = 1e-5
MESH = pl.DeviceIdType.MESH
F32 = jnp.float32
BF16 = jnp.bfloat16


class Sems:
    def __init__(self):
        self.count = 0

    def take(self, n):
        base = self.count
        self.count += n
        return base


def layout(n_chip, n_row, n_col):
    sems = Sems()
    names = dict(st1=n_row, st2=n_row, qd=3 * n_chip, qi=3 * n_chip, ag=n_row, wo=n_col,
                 fd=n_chip, fi=n_chip, ug=n_row, fo=n_col)
    table = {name: sems.take(n) for name, n in names.items()}
    return table, sems.count


def kernel(dims, hid_hbm, len_hbm, kc_hbm, vc_hbm, g1_hbm, b1_hbm, wq_hbm, bq_hbm, wk_hbm, bk_hbm, wv_hbm, bv_hbm,
           wo_hbm, bo_hbm, g2_hbm, b2_hbm, w1_hbm, bf1_hbm, w2_hbm, bf2_hbm,
           h_out, k_out, v_out,
           hid_v, len_v, kc, vc, g1, b1, wq, bq, wk, bk, wv, bv, wo, bo, g2, b2, w1, bf1, w2, bf2,
           state, st_send, st_recv, qd_send, qd_recv, q_mine, qi_send, qi_recv, ag_send, ag_recv, wo_recv,
           fd_send, fd_recv, f_mine, fi_send, fi_recv, ug_recv, fo_recv,
           small_sem, big_sem, ssem, rsem):
    n_layer, n_row, n_col, table = dims
    n_chip = n_row // 2
    row = lax.axis_index("row")
    col = lax.axis_index("col")
    chip = row // 2
    par = row % 2
    partner = row + 1 - 2 * par
    batch, width = hid_v.shape
    full = width * n_row
    hd = kc.shape[-1]
    keys = kc.shape[2]
    ffb = fd_send.shape[-1]
    offs = [2, 1, 3, 0]

    small = [(hid_hbm, hid_v), (len_hbm, len_v), (g1_hbm, g1), (b1_hbm, b1), (bq_hbm, bq), (bk_hbm, bk),
             (bv_hbm, bv), (bo_hbm, bo), (g2_hbm, g2), (b2_hbm, b2), (bf1_hbm, bf1), (bf2_hbm, bf2)]
    small_copies = [pltpu.make_async_copy(s, d, small_sem.at[i]) for i, (s, d) in enumerate(small)]
    for c in small_copies:
        c.start()

    bigs = [(wq_hbm, wq), (wk_hbm, wk), (wv_hbm, wv), (kc_hbm, kc), (vc_hbm, vc), (wo_hbm, wo), (w1_hbm, w1),
            (w2_hbm, w2)]
    WQ, WK, WV, KC, VC, WO, W1, W2 = range(8)

    def big_copy(i, l):
        s, d = bigs[i]
        src = s.at[l, :, 0] if i in (KC, VC) else s.at[l]
        return pltpu.make_async_copy(src, d.at[l], big_sem.at[l, i])

    for l in range(n_layer):
        for i in range(8):
            big_copy(i, l).start()

    barrier = pltpu.get_barrier_semaphore()
    for t in range(1, n_row):
        pl.semaphore_signal(barrier, inc=1, device_id={"row": lax.rem(row + t, n_row)}, device_id_type=MESH)
    for t in range(1, n_col):
        pl.semaphore_signal(barrier, inc=1, device_id={"col": lax.rem(col + t, n_col)}, device_id_type=MESH)
    for c in small_copies:
        c.wait()
    state[...] = hid_v[...]
    pl.semaphore_wait(barrier, n_row - 1 + n_col - 1)

    def remote(l, name, i_send, i_recv, src, dst, axis, target):
        return pltpu.make_async_remote_copy(
            src_ref=src, dst_ref=dst, send_sem=ssem.at[l, table[name] + i_send], recv_sem=rsem.at[l, table[name] + i_recv],
            device_id={axis: target}, device_id_type=MESH)

    def pick(ref, l):
        rows = ref[...].astype(F32)
        out = rows[0:1]
        for i in range(1, n_layer):
            out = jnp.where(l == i, rows[i:i + 1], out)
        return out

    def pick_slice(ref, l, start, size):
        rows = ref[:, pl.ds(pl.multiple_of(start, size), size)].astype(F32)
        out = rows[0:1]
        for i in range(1, n_layer):
            out = jnp.where(l == i, rows[i:i + 1], out)
        return out

    eye = lax.broadcasted_iota(jnp.int32, (batch, 128), 0) == lax.broadcasted_iota(jnp.int32, (batch, 128), 1)
    lens = jnp.sum(jnp.where(eye, jnp.pad(len_v[...], ((0, 0), (0, 128 - batch))), 0), axis=1, keepdims=True)

    row_order = []
    for off in offs[:-1]:
        k = lax.rem(chip + off, n_chip)
        row_order += [2 * k + par, 2 * k + 1 - par]
    row_order.append(partner)

    def layer_norm(l, name, which, gain, shift):
        x = state[...].astype(F32)
        s1 = jnp.sum(x, axis=1, keepdims=True)
        s2 = jnp.sum(x * x, axis=1, keepdims=True)
        r1 = jnp.sum(jnp.where(eye, s1, 0.0), axis=0, keepdims=True)
        r2 = jnp.sum(jnp.where(eye, s2, 0.0), axis=0, keepdims=True)
        sub = lax.broadcasted_iota(jnp.int32, (8, 128), 0)
        tile = jnp.where(sub == 0, r1, jnp.where(sub == 1, r2, 0.0))
        st_send[l, which] = tile
        st_recv[l, which, row] = tile
        for t, j in enumerate(row_order):
            remote(l, name, t, row, st_send.at[l, which], st_recv.at[l, which, row], "row", j).start()
        for t, j in enumerate(row_order):
            remote(l, name, t, j, st_send.at[l, which], st_recv.at[l, which, j], "row", j).wait_recv()
        tot = jnp.sum(st_recv[l, which], axis=0)
        m = jnp.sum(jnp.where(eye, tot[0:1], 0.0), axis=1, keepdims=True) / full
        var = jnp.sum(jnp.where(eye, tot[1:2], 0.0), axis=1, keepdims=True) / full - m * m
        y = (x - m) * lax.rsqrt(var + EPS_LN) * pick(gain, l) + pick(shift, l)
        return y.astype(BF16)

    def ar_col(l, name, part, buf, bias):
        buf[l, col] = part.astype(BF16)
        for t in (2, 1, 3):
            j = lax.rem(col + t, n_col)
            remote(l, name, t, col, buf.at[l, col], buf.at[l, col], "col", j).start()
        for t in (1, 3, 2):
            j = lax.rem(col + t, n_col)
            remote(l, name, t, j, buf.at[l, col], buf.at[l, j], "col", j).wait_recv()
        total = buf[l, 0].astype(F32)
        for j in range(1, n_col):
            total = total + buf[l, j].astype(F32)
        state[...] = (state[...].astype(F32) + (total + bias)).astype(BF16)

    def layer(l, carry):
        y = layer_norm(l, "st1", 0, g1, b1)

        def project(w, i_big, wref):
            big_copy(i_big, l).wait()
            for off in offs:
                k = lax.rem(chip + off, n_chip)
                res = jnp.dot(y, wref[l, :, pl.ds(pl.multiple_of(k * 2 * hd, 2 * hd), 2 * hd)],
                              preferred_element_type=F32)
                lo, hi = res[:, :hd], res[:, hd:]
                qd_send[l, w, k] = jnp.where(par == 0, hi, lo).astype(BF16)
                q_mine[w, k] = jnp.where(par == 0, lo, hi)
                remote(l, "qd", w * n_chip + k, w * n_chip + k, qd_send.at[l, w, k], qd_recv.at[l, w, k],
                       "row", partner).start()

        def forward(w):
            for off in offs:
                k = lax.rem(chip + off, n_chip)
                remote(l, "qd", w * n_chip + k, w * n_chip + k, qd_send.at[l, w, k], qd_recv.at[l, w, k],
                       "row", partner).wait_recv()
                both = q_mine[w, k] + qd_recv[l, w, k].astype(F32)
                if off:
                    qi_send[l, w, k] = both.astype(BF16)
                    remote(l, "qi", w * n_chip + k, w * n_chip + chip, qi_send.at[l, w, k], qi_recv.at[l, w, chip],
                           "row", 2 * k + par).start()
                else:
                    q_mine[w, k] = both

        def collect(w, bias):
            total = q_mine[w, chip]
            for off in (1, 3, 2):
                k = lax.rem(chip + off, n_chip)
                remote(l, "qi", w * n_chip + k, w * n_chip + k, qi_send.at[l, w, k], qi_recv.at[l, w, k],
                       "row", 2 * k + par).wait_recv()
                total = total + qi_recv[l, w, k].astype(F32)
            return total + pick_slice(bias, l, row * hd, hd)

        project(0, WQ, wq)
        project(1, WK, wk)
        forward(0)
        project(2, WV, wv)
        forward(1)
        forward(2)
        q = (collect(0, bq) * (hd ** -0.5)).astype(BF16).astype(F32)

        group = 16
        rowi = lax.broadcasted_iota(jnp.int32, (group, 1), 0)
        big_copy(KC, l).wait()
        parts = []
        for g in range(batch // group):
            q_g = q[g * group:(g + 1) * group]
            lhs = jnp.concatenate([jnp.where(rowi == i, q_g, 0.0) for i in range(group)], axis=1).astype(BF16)
            k_g = jnp.concatenate([kc[l, g * group + i] for i in range(group)], axis=1)
            parts.append(lax.dot_general(lhs, k_g, (((1,), (1,)), ((), ())), preferred_element_type=F32))
        scores = jnp.concatenate(parts, axis=0)
        scores = jnp.where(lax.broadcasted_iota(jnp.int32, (batch, keys), 1) < lens, scores, -jnp.inf)
        k_new = collect(1, bk).astype(BF16)
        k_out[l] = k_new
        s_new = jnp.sum(q * k_new.astype(F32), axis=1, keepdims=True)
        peak = jnp.maximum(jnp.max(scores, axis=1, keepdims=True), s_new)
        e = jnp.exp(scores - peak)
        e_new = jnp.exp(s_new - peak)
        mass = jnp.sum(e, axis=1, keepdims=True) + e_new
        prob = (e / mass).astype(BF16).astype(F32)
        prob_new = (e_new / mass).astype(BF16).astype(F32)
        big_copy(VC, l).wait()
        outs = []
        for g in range(batch // group):
            p_g = prob[g * group:(g + 1) * group]
            lhs = jnp.concatenate([jnp.where(rowi // 2 == i, p_g, 0.0) for i in range(group // 2)],
                                  axis=1).astype(BF16)
            v_g = jnp.concatenate([jnp.concatenate([vc[l, g * group + 2 * i], vc[l, g * group + 2 * i + 1]], axis=1)
                                   for i in range(group // 2)], axis=0)
            out = jnp.dot(lhs, v_g, preferred_element_type=F32)
            outs.append(jnp.where(rowi % 2 == 0, out[:, :hd], out[:, hd:]))
        v_new = collect(2, bv).astype(BF16)
        v_out[l] = v_new
        mixed = jnp.concatenate(outs, axis=0) + prob_new * v_new.astype(F32)

        ag_recv[l, row] = mixed.astype(BF16)
        for t, j in enumerate(row_order):
            remote(l, "ag", t, row, ag_recv.at[l, row], ag_recv.at[l, row], "row", j).start()
        big_copy(WO, l).wait()
        for t, j in enumerate(row_order):
            remote(l, "ag", t, j, ag_recv.at[l, row], ag_recv.at[l, j], "row", j).wait_recv()
        gathered = jnp.concatenate([ag_recv[l, j] for j in range(n_row)], axis=1)
        ar_col(l, "wo", jnp.dot(gathered, wo[l], preferred_element_type=F32), wo_recv, pick(bo, l))

        y2 = layer_norm(l, "st2", 1, g2, b2)
        big_copy(W1, l).wait()

        def fc1_block(j):
            return jnp.dot(y2, w1[l, :, pl.ds(pl.multiple_of(j * ffb, ffb), ffb)], preferred_element_type=F32)

        for off in offs:
            k = lax.rem(chip + off, n_chip)
            fd_send[l, k] = fc1_block(2 * k + 1 - par).astype(BF16)
            remote(l, "fd", k, k, fd_send.at[l, k], fd_recv.at[l, k], "row", partner).start()
        for off in offs:
            k = lax.rem(chip + off, n_chip)
            f_mine[k] = fc1_block(2 * k + par)
        for off in offs:
            k = lax.rem(chip + off, n_chip)
            remote(l, "fd", k, k, fd_send.at[l, k], fd_recv.at[l, k], "row", partner).wait_recv()
            both = f_mine[k] + fd_recv[l, k].astype(F32)
            if off:
                fi_send[l, k] = both.astype(BF16)
                remote(l, "fi", k, chip, fi_send.at[l, k], fi_recv.at[l, chip], "row", 2 * k + par).start()
            else:
                f_mine[k] = both
        total = f_mine[chip]
        for off in (1, 3, 2):
            k = lax.rem(chip + off, n_chip)
            remote(l, "fi", k, k, fi_send.at[l, k], fi_recv.at[l, k], "row", 2 * k + par).wait_recv()
            total = total + fi_recv[l, k].astype(F32)
        u = jnp.maximum((total + pick_slice(bf1, l, row * ffb, ffb)).astype(BF16), 0)

        ug_recv[l, row] = u
        for off in offs[:-1]:
            k = lax.rem(chip + off, n_chip)
            remote(l, "ug", 2 * k + par, row, ug_recv.at[l, row], ug_recv.at[l, row], "row", 2 * k + par).start()
        remote(l, "ug", row, row, ug_recv.at[l, row], ug_recv.at[l, row], "row", partner).start()
        big_copy(W2, l).wait()

        def fc2_block(j, u_j):
            return jnp.dot(u_j, w2[l, pl.ds(pl.multiple_of(j * ffb, ffb), ffb), :], preferred_element_type=F32)

        acc = fc2_block(row, u)

        def got(j, target):
            remote(l, "ug", j, j, ug_recv.at[l, row], ug_recv.at[l, j], "row", target).wait_recv()

        got(partner, partner)
        acc = acc + fc2_block(partner, ug_recv[l, partner])
        for off in (1, 3, 2):
            k = lax.rem(chip + off, n_chip)
            j = 2 * k + par
            got(j, j)
            remote(l, "ug", 2 * k + 1 - par, j, ug_recv.at[l, j], ug_recv.at[l, j], "row", partner).start()
            acc = acc + fc2_block(j, ug_recv[l, j])
        for off in (1, 3, 2):
            k = lax.rem(chip + off, n_chip)
            j = 2 * k + 1 - par
            got(j, partner)
            acc = acc + fc2_block(j, ug_recv[l, j])
        ar_col(l, "fo", acc, fo_recv, pick(bf2, l))
        return carry

    lax.fori_loop(0, n_layer, layer, 0)
    h_out[...] = state[...]

    def drain(l, carry):
        def done(name, i, src, axis, target):
            remote(l, name, i, i, src, src, axis, target).wait_send()

        for t, j in enumerate(row_order):
            done("st1", t, st_send.at[l, 0], "row", j)
            done("st2", t, st_send.at[l, 1], "row", j)
            done("ag", t, ag_recv.at[l, row], "row", j)
        for t in (1, 2, 3):
            j = lax.rem(col + t, n_col)
            done("wo", t, wo_recv.at[l, col], "col", j)
            done("fo", t, fo_recv.at[l, col], "col", j)
        for off in offs:
            k = lax.rem(chip + off, n_chip)
            for w in range(3):
                done("qd", w * n_chip + k, qd_send.at[l, w, k], "row", partner)
                if off:
                    done("qi", w * n_chip + k, qi_send.at[l, w, k], "row", 2 * k + par)
            done("fd", k, fd_send.at[l, k], "row", partner)
            if off:
                done("fi", k, fi_send.at[l, k], "row", 2 * k + par)
                done("ug", 2 * k + par, ug_recv.at[l, row], "row", 2 * k + par)
                done("ug", 2 * k + 1 - par, ug_recv.at[l, 2 * k + par], "row", partner)
            else:
                done("ug", row, ug_recv.at[l, row], "row", partner)
        return carry

    lax.fori_loop(0, n_layer, drain, 0)


def solution(mesh):
    n_row, n_col = mesh.shape["row"], mesh.shape["col"]
    n_chip = n_row // 2
    act_spec = P("dp", "row")
    cache_spec = P(None, "dp", ("col", "row"), None, None)
    fresh_spec = P(None, "dp", ("col", "row"), None)
    in_weight = P(None, "row", "col")
    out_weight = P(None, "col", "row")
    col_vec = P(None, "col")
    row_vec = P(None, "row")
    in_specs = (act_spec, P("dp"), cache_spec, cache_spec, row_vec, row_vec,
                in_weight, col_vec, in_weight, col_vec, in_weight, col_vec,
                out_weight, row_vec, row_vec, row_vec, in_weight, col_vec, out_weight, row_vec)

    def local_step(hidden, cache_len, k_cache, v_cache, ln1_g, ln1_b, w_q, b_q, w_k, b_k, w_v, b_v,
                   w_o, b_o, ln2_g, ln2_b, w_fc1, b_fc1, w_fc2, b_fc2):
        batch, width = hidden.shape
        n_layer, _, _, keys, hd = k_cache.shape
        ff = w_fc1.shape[2]
        ffb = ff // n_row
        table, n_sem = layout(n_chip, n_row, n_col)
        args = (hidden, cache_len.reshape(1, batch), k_cache, v_cache, ln1_g, ln1_b, w_q, b_q, w_k, b_k, w_v, b_v,
                w_o, b_o, ln2_g, ln2_b, w_fc1, b_fc1, w_fc2, b_fc2)

        def vm(shape, dtype=BF16):
            return pltpu.VMEM(shape, dtype)

        local = [vm(a.shape, a.dtype) for a in args]
        local[2] = local[3] = vm((n_layer, batch, keys, hd))
        scratch = local + [
            vm((batch, width)),
            vm((n_layer, 2, 8, 128), F32), vm((n_layer, 2, n_row, 8, 128), F32),
            vm((n_layer, 3, n_chip, batch, hd)), vm((n_layer, 3, n_chip, batch, hd)),
            vm((3, n_chip, batch, hd), F32),
            vm((n_layer, 3, n_chip, batch, hd)), vm((n_layer, 3, n_chip, batch, hd)),
            vm((8, 128)), vm((n_layer, n_row, batch, hd)),
            vm((n_layer, n_col, batch, width)),
            vm((n_layer, n_chip, batch, ffb)), vm((n_layer, n_chip, batch, ffb)), vm((n_chip, batch, ffb), F32),
            vm((n_layer, n_chip, batch, ffb)), vm((n_layer, n_chip, batch, ffb)),
            vm((n_layer, n_row, batch, ffb)),
            vm((n_layer, n_col, batch, width)),
            pltpu.SemaphoreType.DMA((12,)), pltpu.SemaphoreType.DMA((n_layer, 8)),
            pltpu.SemaphoreType.DMA((n_layer, n_sem)), pltpu.SemaphoreType.DMA((n_layer, n_sem)),
        ]
        out_shape = (jax.ShapeDtypeStruct((batch, width), BF16),
                     jax.ShapeDtypeStruct((n_layer, batch, hd), BF16),
                     jax.ShapeDtypeStruct((n_layer, batch, hd), BF16))
        h_out, k_new, v_new = pl.pallas_call(
            functools.partial(kernel, (n_layer, n_row, n_col, table)),
            out_shape=out_shape,
            in_specs=[pl.BlockSpec(memory_space=pl.ANY)] * len(args),
            out_specs=[pl.BlockSpec(memory_space=pltpu.VMEM)] * 3,
            scratch_shapes=scratch,
            compiler_params=pltpu.CompilerParams(collective_id=0, has_side_effects=True,
                                                 vmem_limit_bytes=66 * 1000 * 1000),
        )(*args)
        return h_out, k_new[:, :, None, :], v_new[:, :, None, :]

    return jax.shard_map(local_step, mesh=mesh, in_specs=in_specs,
                         out_specs=(act_spec, fresh_spec, fresh_spec), check_vma=False)
```

time: 571 us -> 111 us (0.19)
  waiting for transfers between devices: 401 us -> 0 us
  Pallas kernels: 0 us -> 105 us
  blocking collectives: 95.2 us -> 0 us
  matrix products: 36.9 us -> 0 us
  between operations: 14.7 us -> 0.65 us
  other arithmetic: 9.87 us -> 0 us
  local copies, waits for them, and re-layouts: 10.1 us -> 4.22 us
    psum x6 -> x0, waiting for transfers between devices: 254 us -> none  [the longest x2 103 us: local_step(): inner_sum = lax.psum(inner_part, 'row')]
    unnamed x18 -> x0, waiting for transfers between devices: 147 us -> none
    pallas_call x0 -> x1, Pallas kernels: none -> 105 us  [local_step(): pl.pallas_call(functools.partial(kernel, (n_layer, n_row, n_col, table)),...]
    psum x4 -> x0, blocking collectives: 57.3 us -> none  [layer_norm(): stats = lax.psum(stats, 'row')]
    all_gather x2 -> x0, blocking collectives: 37.8 us -> none  [local_step(): lax.all_gather(attended.reshape(batch_rows, heads_dev * head_dim), 'row',...]
    dot_general x16 -> x0, matrix products: 36.9 us -> none  [the longest x2 7.8 us: local_step(): jnp.dot(normed_two, w_fc1[layer], preferred_element_type=jnp.float32)]
    unnamed x40 -> x3, local copies, waits for them, and re-layouts: 10.1 us -> 4.22 us
  transfers between devices with their start and end apart: 12 -> 0, of which waited for: 12 -> 0; matrix products, arithmetic and copies ran while one was open for 4% -> 0% of each run, Pallas kernels for 0% -> 0%
where the time goes in v1:
time: 111 us; the launch traced here: 110 us
  Pallas kernels  105 us (95%)
  local copies, waits for them, and re-layouts  4.22 us (4%)
    pallas_call x1, Pallas kernels, local_step(): pl.pallas_call(functools.partial(kernel, (n_layer, n_row, n_col, table)),...  105 us
    unnamed x3, local copies, waits for them, and re-layouts  4.22 us

profile of v1, /device:TPU:97, one launch (start us, length us, event | category | flops | bytes accessed | tf_op | source)
XLA Modules:
  0.0 110.3 jit_solution(3284041560754687427)
XLA Ops:
  0.6 105.4 %shard_map.211 = (bf16[64,512]{1,0:T(8,128)(2,1)}, bf16[2,64,128]{2,1,0:T(8,128)(2,1)}, bf16[2,64,128]{2,1,0:T(8,128)(2,1)}) custom-call(bf16[64,512]{1,0:T(8,128)(2,1)} %hid_hbm.1, s32[1,64]{1,0:T(1,128)} %bitcast.9, bf16[2,64,1,256,128]{4,3,2,1,0:T(8,128)(2,1)} %kc_hbm.1, bf16[2,64,1,256,128]{4,3,2,1,0:T(8,128)(2,1)} %vc_hbm.1, bf16[2,512]{1,0:T(2,128)(2,1)} %g1_hbm.1, ...), custom_call_target="tpu_custom_call" | custom-call | tf_op jit(solution)/shard_map/pallas_call | solution.py:373
  106.1 1.5 %copy.28 = bf16[64,512]{1,0:T(8,128)(2,1)} copy(bf16[64,512]{1,0:T(8,128)(2,1)} %get-tuple-element.15) | data formatting | bytes 131072
  107.5 1.4 %copy.29 = bf16[2,64,1,128]{3,1,2,0:T(8,128)(2,1)} copy(bf16[2,64,1,128]{3,1,2,0:T(8,128)(2,1)} %bitcast.8) | data formatting | bytes 65536
  108.9 1.4 %copy.30 = bf16[2,64,1,128]{3,1,2,0:T(8,128)(2,1)} copy(bf16[2,64,1,128]{3,1,2,0:T(8,128)(2,1)} %bitcast.7) | data formatting | bytes 65536

commit v2 on v1

--- a/solution.py
+++ b/solution.py
@@ -25,7 +25,7 @@
 
 def layout(n_chip, n_row, n_col):
     sems = Sems()
-    names = dict(st1=n_row, st2=n_row, qd=3 * n_chip, qi=3 * n_chip, ag=n_row, wo=n_col,
+    names = dict(st1=n_row, st2=n_row, qd=3, qi=3 * n_chip, ag=n_row, wo=n_col,
                  fd=n_chip, fi=n_chip, ug=n_row, fo=n_col)
     table = {name: sems.take(n) for name, n in names.items()}
     return table, sems.count
@@ -35,9 +35,9 @@
            wo_hbm, bo_hbm, g2_hbm, b2_hbm, w1_hbm, bf1_hbm, w2_hbm, bf2_hbm,
            h_out, k_out, v_out,
            hid_v, len_v, kc, vc, g1, b1, wq, bq, wk, bk, wv, bv, wo, bo, g2, b2, w1, bf1, w2, bf2,
-           state, st_send, st_recv, qd_send, qd_recv, q_mine, qi_send, qi_recv, ag_send, ag_recv, wo_recv,
-           fd_send, fd_recv, f_mine, fi_send, fi_recv, ug_recv, fo_recv,
-           small_sem, big_sem, ssem, rsem):
+           state, st_send, st_recv, qd_send, qd_recv, q_mine, q_own, qi_send, qi_recv, k_stage, v_stage, ag_recv, wo_recv,
+           fd_send, fd_recv, f_mine, f_own, fi_send, fi_recv, ug_recv, fo_recv,
+           small_sem, big_sem, out_sem, ssem, rsem):
     n_layer, n_row, n_col, table = dims
     n_chip = n_row // 2
     row = lax.axis_index("row")
@@ -46,7 +46,6 @@
     par = row % 2
     partner = row + 1 - 2 * par
     batch, width = hid_v.shape
-    full = width * n_row
     hd = kc.shape[-1]
     keys = kc.shape[2]
     ffb = fd_send.shape[-1]
@@ -67,9 +66,8 @@
         src = s.at[l, :, 0] if i in (KC, VC) else s.at[l]
         return pltpu.make_async_copy(src, d.at[l], big_sem.at[l, i])
 
-    for l in range(n_layer):
-        for i in range(8):
-            big_copy(i, l).start()
+    for i in (WQ, WK, WV):
+        big_copy(i, 0).start()
 
     barrier = pltpu.get_barrier_semaphore()
     for t in range(1, n_row):
@@ -79,6 +77,11 @@
     for c in small_copies:
         c.wait()
     state[...] = hid_v[...]
+    for i in (KC, VC, WO, W1, W2):
+        big_copy(i, 0).start()
+    for l in range(1, n_layer):
+        for i in range(8):
+            big_copy(i, l).start()
     pl.semaphore_wait(barrier, n_row - 1 + n_col - 1)
 
     def remote(l, name, i_send, i_recv, src, dst, axis, target):
@@ -109,25 +112,56 @@
         row_order += [2 * k + par, 2 * k + 1 - par]
     row_order.append(partner)
 
-    def layer_norm(l, name, which, gain, shift):
+    def to_row(column):
+        return jnp.sum(jnp.where(eye, column, 0.0), axis=0, keepdims=True)
+
+    def to_column(line):
+        return jnp.sum(jnp.where(eye, line, 0.0), axis=1, keepdims=True)
+
+    def local_norm(l, name, which, gain, shift):
         x = state[...].astype(F32)
-        s1 = jnp.sum(x, axis=1, keepdims=True)
-        s2 = jnp.sum(x * x, axis=1, keepdims=True)
-        r1 = jnp.sum(jnp.where(eye, s1, 0.0), axis=0, keepdims=True)
-        r2 = jnp.sum(jnp.where(eye, s2, 0.0), axis=0, keepdims=True)
+        c = jnp.sum(x, axis=1, keepdims=True) / width
+        xc = x - c
+        v = jnp.sum(xc * xc, axis=1, keepdims=True) / width
         sub = lax.broadcasted_iota(jnp.int32, (8, 128), 0)
-        tile = jnp.where(sub == 0, r1, jnp.where(sub == 1, r2, 0.0))
+        tile = jnp.where(sub == 0, to_row(c), jnp.where(sub == 1, to_row(v), 0.0))
         st_send[l, which] = tile
         st_recv[l, which, row] = tile
         for t, j in enumerate(row_order):
             remote(l, name, t, row, st_send.at[l, which], st_recv.at[l, which, row], "row", j).start()
+        g, b = pick(gain, l), pick(shift, l)
+        y = xc * lax.rsqrt(v + EPS_LN) * g
+        extra = lax.broadcasted_iota(jnp.int32, (16, 1), 0)
+        extra = jnp.where(extra == 0, g, jnp.where(extra == 1, b, 0.0))
+        return jnp.concatenate([y.astype(BF16), extra.astype(BF16)], axis=0)
+
+    def global_norm(l, name, which):
         for t, j in enumerate(row_order):
             remote(l, name, t, j, st_send.at[l, which], st_recv.at[l, which, j], "row", j).wait_recv()
-        tot = jnp.sum(st_recv[l, which], axis=0)
-        m = jnp.sum(jnp.where(eye, tot[0:1], 0.0), axis=1, keepdims=True) / full
-        var = jnp.sum(jnp.where(eye, tot[1:2], 0.0), axis=1, keepdims=True) / full - m * m
-        y = (x - m) * lax.rsqrt(var + EPS_LN) * pick(gain, l) + pick(shift, l)
-        return y.astype(BF16)
+        m = jnp.zeros((1, 128), F32)
+        for j in range(n_row):
+            m = m + st_recv[l, which, j][0:1]
+        m = m / n_row
+        var = jnp.zeros((1, 128), F32)
+        for j in range(n_row):
+            tile = st_recv[l, which, j]
+            var = var + (tile[1:2] + (tile[0:1] - m) * (tile[0:1] - m))
+        r = lax.rsqrt(var / n_row + EPS_LN)
+
+        def coefficients(tile):
+            local = tile[1:2] + EPS_LN
+            return to_column(r * (local * lax.rsqrt(local))), to_column(r * (tile[0:1] - m))
+
+        mine = coefficients(st_recv[l, which, row])
+        other = coefficients(st_recv[l, which, partner])
+
+        def combine(own, got):
+            got = got.astype(F32)
+            return ((mine[0] * own[:batch] + other[0] * got[:batch])
+                    + (mine[1] * own[batch:batch + 1] + other[1] * got[batch:batch + 1])
+                    + (own[batch + 1:batch + 2] + got[batch + 1:batch + 2]))
+
+        return combine
 
     def ar_col(l, name, part, buf, bias):
         buf[l, col] = part.astype(BF16)
@@ -143,35 +177,36 @@
         state[...] = (state[...].astype(F32) + (total + bias)).astype(BF16)
 
     def layer(l, carry):
-        y = layer_norm(l, "st1", 0, g1, b1)
+        y = local_norm(l, "st1", 0, g1, b1)
+
+        def pair(w):
+            return remote(l, "qd", w, w, qd_send.at[l, w], qd_recv.at[l, w], "row", partner)
 
         def project(w, i_big, wref):
             big_copy(i_big, l).wait()
-            for off in offs:
+            res = jnp.dot(y, wref[l], preferred_element_type=F32)
+            even = jnp.concatenate([res[:, 2 * k * hd:(2 * k + 1) * hd] for k in range(n_chip)], axis=1)
+            odd = jnp.concatenate([res[:, (2 * k + 1) * hd:(2 * k + 2) * hd] for k in range(n_chip)], axis=1)
+            qd_send[l, w] = jnp.where(par == 0, odd, even).astype(BF16)
+            pair(w).start()
+            q_mine[w] = jnp.where(par == 0, even, odd)
+
+        def forward(w):
+            pair(w).wait_recv()
+            both = combine(q_mine[w], qd_recv[l, w])
+            own = both[:, :hd]
+            for k in range(n_chip):
+                block = both[:, k * hd:(k + 1) * hd]
+                own = jnp.where(chip == k, block, own)
+                qi_send[l, w, k] = block.astype(BF16)
+            for off in offs[:-1]:
                 k = lax.rem(chip + off, n_chip)
-                res = jnp.dot(y, wref[l, :, pl.ds(pl.multiple_of(k * 2 * hd, 2 * hd), 2 * hd)],
-                              preferred_element_type=F32)
-                lo, hi = res[:, :hd], res[:, hd:]
-                qd_send[l, w, k] = jnp.where(par == 0, hi, lo).astype(BF16)
-                q_mine[w, k] = jnp.where(par == 0, lo, hi)
-                remote(l, "qd", w * n_chip + k, w * n_chip + k, qd_send.at[l, w, k], qd_recv.at[l, w, k],
-                       "row", partner).start()
-
-        def forward(w):
-            for off in offs:
-                k = lax.rem(chip + off, n_chip)
-                remote(l, "qd", w * n_chip + k, w * n_chip + k, qd_send.at[l, w, k], qd_recv.at[l, w, k],
-                       "row", partner).wait_recv()
-                both = q_mine[w, k] + qd_recv[l, w, k].astype(F32)
-                if off:
-                    qi_send[l, w, k] = both.astype(BF16)
-                    remote(l, "qi", w * n_chip + k, w * n_chip + chip, qi_send.at[l, w, k], qi_recv.at[l, w, chip],
-                           "row", 2 * k + par).start()
-                else:
-                    q_mine[w, k] = both
+                remote(l, "qi", w * n_chip + k, w * n_chip + chip, qi_send.at[l, w, k], qi_recv.at[l, w, chip],
+                       "row", 2 * k + par).start()
+            q_own[w] = own
 
         def collect(w, bias):
-            total = q_mine[w, chip]
+            total = q_own[w]
             for off in (1, 3, 2):
                 k = lax.rem(chip + off, n_chip)
                 remote(l, "qi", w * n_chip + k, w * n_chip + k, qi_send.at[l, w, k], qi_recv.at[l, w, k],
@@ -181,8 +216,9 @@
 
         project(0, WQ, wq)
         project(1, WK, wk)
+        project(2, WV, wv)
+        combine = global_norm(l, "st1", 0)
         forward(0)
-        project(2, WV, wv)
         forward(1)
         forward(2)
         q = (collect(0, bq) * (hd ** -0.5)).astype(BF16).astype(F32)
@@ -199,7 +235,8 @@
         scores = jnp.concatenate(parts, axis=0)
         scores = jnp.where(lax.broadcasted_iota(jnp.int32, (batch, keys), 1) < lens, scores, -jnp.inf)
         k_new = collect(1, bk).astype(BF16)
-        k_out[l] = k_new
+        k_stage[l] = k_new
+        pltpu.make_async_copy(k_stage.at[l], k_out.at[l], out_sem.at[l, 0]).start()
         s_new = jnp.sum(q * k_new.astype(F32), axis=1, keepdims=True)
         peak = jnp.maximum(jnp.max(scores, axis=1, keepdims=True), s_new)
         e = jnp.exp(scores - peak)
@@ -218,7 +255,8 @@
             out = jnp.dot(lhs, v_g, preferred_element_type=F32)
             outs.append(jnp.where(rowi % 2 == 0, out[:, :hd], out[:, hd:]))
         v_new = collect(2, bv).astype(BF16)
-        v_out[l] = v_new
+        v_stage[l] = v_new
+        pltpu.make_async_copy(v_stage.at[l], v_out.at[l], out_sem.at[l, 1]).start()
         mixed = jnp.concatenate(outs, axis=0) + prob_new * v_new.astype(F32)
 
         ag_recv[l, row] = mixed.astype(BF16)
@@ -230,7 +268,7 @@
         gathered = jnp.concatenate([ag_recv[l, j] for j in range(n_row)], axis=1)
         ar_col(l, "wo", jnp.dot(gathered, wo[l], preferred_element_type=F32), wo_recv, pick(bo, l))
 
-        y2 = layer_norm(l, "st2", 1, g2, b2)
+        y2 = local_norm(l, "st2", 1, g2, b2)
         big_copy(W1, l).wait()
 
         def fc1_block(j):
@@ -243,16 +281,17 @@
         for off in offs:
             k = lax.rem(chip + off, n_chip)
             f_mine[k] = fc1_block(2 * k + par)
+        combine = global_norm(l, "st2", 1)
         for off in offs:
             k = lax.rem(chip + off, n_chip)
             remote(l, "fd", k, k, fd_send.at[l, k], fd_recv.at[l, k], "row", partner).wait_recv()
-            both = f_mine[k] + fd_recv[l, k].astype(F32)
+            both = combine(f_mine[k], fd_recv[l, k])
             if off:
                 fi_send[l, k] = both.astype(BF16)
                 remote(l, "fi", k, chip, fi_send.at[l, k], fi_recv.at[l, chip], "row", 2 * k + par).start()
             else:
-                f_mine[k] = both
-        total = f_mine[chip]
+                f_own[...] = both
+        total = f_own[...]
         for off in (1, 3, 2):
             k = lax.rem(chip + off, n_chip)
             remote(l, "fi", k, k, fi_send.at[l, k], fi_recv.at[l, k], "row", 2 * k + par).wait_recv()
@@ -291,7 +330,7 @@
         return carry
 
     lax.fori_loop(0, n_layer, layer, 0)
-    h_out[...] = state[...]
+    pltpu.make_async_copy(state, h_out, out_sem.at[0, 2]).start()
 
     def drain(l, carry):
         def done(name, i, src, axis, target):
@@ -305,10 +344,13 @@
             j = lax.rem(col + t, n_col)
             done("wo", t, wo_recv.at[l, col], "col", j)
             done("fo", t, fo_recv.at[l, col], "col", j)
+        for w in range(3):
+            done("qd", w, qd_send.at[l, w], "row", partner)
+        pltpu.make_async_copy(k_stage.at[l], k_out.at[l], out_sem.at[l, 0]).wait()
+        pltpu.make_async_copy(v_stage.at[l], v_out.at[l], out_sem.at[l, 1]).wait()
         for off in offs:
             k = lax.rem(chip + off, n_chip)
             for w in range(3):
-                done("qd", w * n_chip + k, qd_send.at[l, w, k], "row", partner)
                 if off:
                     done("qi", w * n_chip + k, qi_send.at[l, w, k], "row", 2 * k + par)
             done("fd", k, fd_send.at[l, k], "row", partner)
@@ -321,6 +363,7 @@
         return carry
 
     lax.fori_loop(0, n_layer, drain, 0)
+    pltpu.make_async_copy(state, h_out, out_sem.at[0, 2]).wait()
 
 
 def solution(mesh):
@@ -355,16 +398,17 @@
         scratch = local + [
             vm((batch, width)),
             vm((n_layer, 2, 8, 128), F32), vm((n_layer, 2, n_row, 8, 128), F32),
+            vm((n_layer, 3, batch + 16, n_chip * hd)), vm((n_layer, 3, batch + 16, n_chip * hd)),
+            vm((3, batch + 16, n_chip * hd), F32), vm((3, batch, hd), F32),
             vm((n_layer, 3, n_chip, batch, hd)), vm((n_layer, 3, n_chip, batch, hd)),
-            vm((3, n_chip, batch, hd), F32),
-            vm((n_layer, 3, n_chip, batch, hd)), vm((n_layer, 3, n_chip, batch, hd)),
-            vm((8, 128)), vm((n_layer, n_row, batch, hd)),
+            vm((n_layer, batch, hd)), vm((n_layer, batch, hd)), vm((n_layer, n_row, batch, hd)),
             vm((n_layer, n_col, batch, width)),
-            vm((n_layer, n_chip, batch, ffb)), vm((n_layer, n_chip, batch, ffb)), vm((n_chip, batch, ffb), F32),
+            vm((n_layer, n_chip, batch + 16, ffb)), vm((n_layer, n_chip, batch + 16, ffb)),
+            vm((n_chip, batch + 16, ffb), F32), vm((batch, ffb), F32),
             vm((n_layer, n_chip, batch, ffb)), vm((n_layer, n_chip, batch, ffb)),
             vm((n_layer, n_row, batch, ffb)),
             vm((n_layer, n_col, batch, width)),
-            pltpu.SemaphoreType.DMA((12,)), pltpu.SemaphoreType.DMA((n_layer, 8)),
+            pltpu.SemaphoreType.DMA((12,)), pltpu.SemaphoreType.DMA((n_layer, 8)), pltpu.SemaphoreType.DMA((n_layer, 3)),
             pltpu.SemaphoreType.DMA((n_layer, n_sem)), pltpu.SemaphoreType.DMA((n_layer, n_sem)),
         ]
         out_shape = (jax.ShapeDtypeStruct((batch, width), BF16),
@@ -374,7 +418,7 @@
             functools.partial(kernel, (n_layer, n_row, n_col, table)),
             out_shape=out_shape,
             in_specs=[pl.BlockSpec(memory_space=pl.ANY)] * len(args),
-            out_specs=[pl.BlockSpec(memory_space=pltpu.VMEM)] * 3,
+            out_specs=[pl.BlockSpec(memory_space=pl.ANY)] * 3,
             scratch_shapes=scratch,
             compiler_params=pltpu.CompilerParams(collective_id=0, has_side_effects=True,
                                                  vmem_limit_bytes=66 * 1000 * 1000),

time: 111 us -> 94.2 us (0.85)
  Pallas kernels: 105 us -> 89.1 us
    pallas_call x1, Pallas kernels: 105 us -> 89.1 us  [local_step(): pl.pallas_call(functools.partial(kernel, (n_layer, n_row, n_col, table)),...]
where the time goes in v2:
time: 94.2 us; the launch traced here: 94 us
  Pallas kernels  89.1 us (95%)
  local copies, waits for them, and re-layouts  4.22 us (4%)
    pallas_call x1, Pallas kernels, local_step(): pl.pallas_call(functools.partial(kernel, (n_layer, n_row, n_col, table)),...  89.1 us
    unnamed x3, local copies, waits for them, and re-layouts  4.22 us

profile of v2, /device:TPU:97, one launch (start us, length us, event | category | flops | bytes accessed | tf_op | source)
XLA Modules:
  0.0 94.0 jit_solution(14806830608969533728)
XLA Ops:
  0.6 89.1 %shard_map.211 = (bf16[64,512]{1,0:T(8,128)(2,1)}, bf16[2,64,128]{2,1,0:T(8,128)(2,1)}, bf16[2,64,128]{2,1,0:T(8,128)(2,1)}) custom-call(bf16[64,512]{1,0:T(8,128)(2,1)} %hid_hbm.1, s32[1,64]{1,0:T(1,128)} %bitcast.9, bf16[2,64,1,256,128]{4,3,2,1,0:T(8,128)(2,1)} %kc_hbm.1, bf16[2,64,1,256,128]{4,3,2,1,0:T(8,128)(2,1)} %vc_hbm.1, bf16[2,512]{1,0:T(2,128)(2,1)} %g1_hbm.1, ...), custom_call_target="tpu_custom_call" | custom-call | tf_op jit(solution)/shard_map/pallas_call | solution.py:417
  89.8 1.5 %copy.28 = bf16[64,512]{1,0:T(8,128)(2,1)} copy(bf16[64,512]{1,0:T(8,128)(2,1)} %get-tuple-element.15) | data formatting | bytes 131072
  91.2 1.4 %copy.29 = bf16[2,64,1,128]{3,1,2,0:T(8,128)(2,1)} copy(bf16[2,64,1,128]{3,1,2,0:T(8,128)(2,1)} %bitcast.8) | data formatting | bytes 65536
  92.6 1.4 %copy.30 = bf16[2,64,1,128]{3,1,2,0:T(8,128)(2,1)} copy(bf16[2,64,1,128]{3,1,2,0:T(8,128)(2,1)} %bitcast.7) | data formatting | bytes 65536

commit v3 on v2

--- a/solution.py
+++ b/solution.py
@@ -25,8 +25,8 @@
 
 def layout(n_chip, n_row, n_col):
     sems = Sems()
-    names = dict(st1=n_row, st2=n_row, qd=3, qi=3 * n_chip, ag=n_row, wo=n_col,
-                 fd=n_chip, fi=n_chip, ug=n_row, fo=n_col)
+    names = dict(st1=n_row, st2=n_row, qi=3 * n_row, ag=n_row, wo=n_col,
+                 fd=n_chip, fi=n_chip, fg=n_chip, ug=n_row, fo=n_col)
     table = {name: sems.take(n) for name, n in names.items()}
     return table, sems.count
 
@@ -35,8 +35,8 @@
            wo_hbm, bo_hbm, g2_hbm, b2_hbm, w1_hbm, bf1_hbm, w2_hbm, bf2_hbm,
            h_out, k_out, v_out,
            hid_v, len_v, kc, vc, g1, b1, wq, bq, wk, bk, wv, bv, wo, bo, g2, b2, w1, bf1, w2, bf2,
-           state, st_send, st_recv, qd_send, qd_recv, q_mine, q_own, qi_send, qi_recv, k_stage, v_stage, ag_recv, wo_recv,
-           fd_send, fd_recv, f_mine, f_own, fi_send, fi_recv, ug_recv, fo_recv,
+           state, st_send, st_recv, qi_send, qi_recv, k_stage, v_stage, ag_recv, wo_recv,
+           fd_send, fd_recv, f_mine, f_own, fi_send, fi_recv, fg_send, fg_recv, ug_recv, fo_recv,
            small_sem, big_sem, out_sem, ssem, rsem):
     n_layer, n_row, n_col, table = dims
     n_chip = n_row // 2
@@ -51,6 +51,12 @@
     ffb = fd_send.shape[-1]
     offs = [2, 1, 3, 0]
 
+    barrier = pltpu.get_barrier_semaphore()
+    for t in range(1, n_row):
+        pl.semaphore_signal(barrier, inc=1, device_id={"row": lax.rem(row + t, n_row)}, device_id_type=MESH)
+    for t in range(1, n_col):
+        pl.semaphore_signal(barrier, inc=1, device_id={"col": lax.rem(col + t, n_col)}, device_id_type=MESH)
+
     small = [(hid_hbm, hid_v), (len_hbm, len_v), (g1_hbm, g1), (b1_hbm, b1), (bq_hbm, bq), (bk_hbm, bk),
              (bv_hbm, bv), (bo_hbm, bo), (g2_hbm, g2), (b2_hbm, b2), (bf1_hbm, bf1), (bf2_hbm, bf2)]
     small_copies = [pltpu.make_async_copy(s, d, small_sem.at[i]) for i, (s, d) in enumerate(small)]
@@ -69,11 +75,6 @@
     for i in (WQ, WK, WV):
         big_copy(i, 0).start()
 
-    barrier = pltpu.get_barrier_semaphore()
-    for t in range(1, n_row):
-        pl.semaphore_signal(barrier, inc=1, device_id={"row": lax.rem(row + t, n_row)}, device_id_type=MESH)
-    for t in range(1, n_col):
-        pl.semaphore_signal(barrier, inc=1, device_id={"col": lax.rem(col + t, n_col)}, device_id_type=MESH)
     for c in small_copies:
         c.wait()
     state[...] = hid_v[...]
@@ -135,33 +136,26 @@
         extra = jnp.where(extra == 0, g, jnp.where(extra == 1, b, 0.0))
         return jnp.concatenate([y.astype(BF16), extra.astype(BF16)], axis=0)
 
-    def global_norm(l, name, which):
-        for t, j in enumerate(row_order):
-            remote(l, name, t, j, st_send.at[l, which], st_recv.at[l, which, j], "row", j).wait_recv()
-        m = jnp.zeros((1, 128), F32)
-        for j in range(n_row):
-            m = m + st_recv[l, which, j][0:1]
-        m = m / n_row
-        var = jnp.zeros((1, 128), F32)
-        for j in range(n_row):
-            tile = st_recv[l, which, j]
-            var = var + (tile[1:2] + (tile[0:1] - m) * (tile[0:1] - m))
-        r = lax.rsqrt(var / n_row + EPS_LN)
-
-        def coefficients(tile):
-            local = tile[1:2] + EPS_LN
-            return to_column(r * (local * lax.rsqrt(local))), to_column(r * (tile[0:1] - m))
-
-        mine = coefficients(st_recv[l, which, row])
-        other = coefficients(st_recv[l, which, partner])
-
-        def combine(own, got):
-            got = got.astype(F32)
-            return ((mine[0] * own[:batch] + other[0] * got[:batch])
-                    + (mine[1] * own[batch:batch + 1] + other[1] * got[batch:batch + 1])
-                    + (own[batch + 1:batch + 2] + got[batch + 1:batch + 2]))
-
-        return combine
+    def wait_stats(l, name, which, sources):
+        for j in sources:
+            remote(l, name, 0, j, st_send.at[l, which], st_recv.at[l, which, j], "row", j).wait_recv()
+
+    def scale_of(v):
+        return (v + EPS_LN) * lax.rsqrt(v + EPS_LN)
+
+    def global_norm(parts):
+        m = sum(c for c, _ in parts) / len(parts)
+        var = sum(v + (c - m) * (c - m) for c, v in parts) / len(parts)
+        r = lax.rsqrt(var + EPS_LN)
+        return [(to_column(r * scale_of(v)), to_column(r * (c - m))) for c, v in parts]
+
+    def stats(l, which, j):
+        tile = st_recv[l, which, j]
+        return tile[0:1], tile[1:2]
+
+    def merge(one, two):
+        half = 0.5 * (one[0] - two[0])
+        return 0.5 * (one[0] + two[0]), 0.5 * (one[1] + two[1]) + half * half
 
     def ar_col(l, name, part, buf, bias):
         buf[l, col] = part.astype(BF16)
@@ -179,48 +173,32 @@
     def layer(l, carry):
         y = local_norm(l, "st1", 0, g1, b1)
 
-        def pair(w):
-            return remote(l, "qd", w, w, qd_send.at[l, w], qd_recv.at[l, w], "row", partner)
-
         def project(w, i_big, wref):
             big_copy(i_big, l).wait()
-            res = jnp.dot(y, wref[l], preferred_element_type=F32)
-            even = jnp.concatenate([res[:, 2 * k * hd:(2 * k + 1) * hd] for k in range(n_chip)], axis=1)
-            odd = jnp.concatenate([res[:, (2 * k + 1) * hd:(2 * k + 2) * hd] for k in range(n_chip)], axis=1)
-            qd_send[l, w] = jnp.where(par == 0, odd, even).astype(BF16)
-            pair(w).start()
-            q_mine[w] = jnp.where(par == 0, even, odd)
-
-        def forward(w):
-            pair(w).wait_recv()
-            both = combine(q_mine[w], qd_recv[l, w])
-            own = both[:, :hd]
-            for k in range(n_chip):
-                block = both[:, k * hd:(k + 1) * hd]
-                own = jnp.where(chip == k, block, own)
-                qi_send[l, w, k] = block.astype(BF16)
-            for off in offs[:-1]:
-                k = lax.rem(chip + off, n_chip)
-                remote(l, "qi", w * n_chip + k, w * n_chip + chip, qi_send.at[l, w, k], qi_recv.at[l, w, chip],
-                       "row", 2 * k + par).start()
-            q_own[w] = own
+            res = jnp.dot(y, wref[l], preferred_element_type=F32).astype(BF16)
+            for j in range(n_row):
+                qi_send[l, w, j] = res[:, j * hd:(j + 1) * hd]
+            for j in row_order:
+                remote(l, "qi", w * n_row + j, w * n_row + row, qi_send.at[l, w, j], qi_recv.at[l, w, row],
+                       "row", j).start()
+            qi_recv[l, w, row] = qi_send[l, w, row]
 
         def collect(w, bias):
-            total = q_own[w]
-            for off in (1, 3, 2):
-                k = lax.rem(chip + off, n_chip)
-                remote(l, "qi", w * n_chip + k, w * n_chip + k, qi_send.at[l, w, k], qi_recv.at[l, w, k],
-                       "row", 2 * k + par).wait_recv()
-                total = total + qi_recv[l, w, k].astype(F32)
-            return total + pick_slice(bias, l, row * hd, hd)
+            for j in row_order:
+                remote(l, "qi", w * n_row + j, w * n_row + j, qi_send.at[l, w, j], qi_recv.at[l, w, j],
+                       "row", j).wait_recv()
+            total = pick_slice(bias, l, row * hd, hd)
+            for j in range(n_row):
+                got = qi_recv[l, w, j].astype(F32)
+                total = total + (coef[j][0] * got[:batch]
+                                 + (coef[j][1] * got[batch:batch + 1] + got[batch + 1:batch + 2]))
+            return total
 
         project(0, WQ, wq)
         project(1, WK, wk)
         project(2, WV, wv)
-        combine = global_norm(l, "st1", 0)
-        forward(0)
-        forward(1)
-        forward(2)
+        wait_stats(l, "st1", 0, row_order)
+        coef = global_norm([stats(l, 0, j) for j in range(n_row)])
         q = (collect(0, bq) * (hd ** -0.5)).astype(BF16).astype(F32)
 
         group = 16
@@ -281,22 +259,57 @@
         for off in offs:
             k = lax.rem(chip + off, n_chip)
             f_mine[k] = fc1_block(2 * k + par)
-        combine = global_norm(l, "st2", 1)
+        wait_stats(l, "st2", 1, [partner])
+        here, there = stats(l, 1, row), stats(l, 1, partner)
+        c_pair, v_pair = merge(here, there)
+        r_pair = lax.rsqrt(v_pair + EPS_LN)
+        a_own, a_got = to_column(r_pair * scale_of(here[1])), to_column(r_pair * scale_of(there[1]))
+        d_own = to_column(r_pair * (here[0] - c_pair))
+        lanes = ffb // 128
         for off in offs:
             k = lax.rem(chip + off, n_chip)
             remote(l, "fd", k, k, fd_send.at[l, k], fd_recv.at[l, k], "row", partner).wait_recv()
-            both = combine(f_mine[k], fd_recv[l, k])
+            own, got = f_mine[k], fd_recv[l, k].astype(F32)
+            g_own, g_got = own[batch:batch + 1], got[batch:batch + 1]
+            both = (a_own * own[:batch] + a_got * got[:batch]) + d_own * (g_own - g_got)
+            rows_gb = jnp.concatenate([g_own + g_got, own[batch + 1:batch + 2] + got[batch + 1:batch + 2]], axis=1)
+            tile = jnp.concatenate([rows_gb[:, i * 128:(i + 1) * 128] for i in range(2 * lanes)], axis=0)
             if off:
                 fi_send[l, k] = both.astype(BF16)
+                fg_send[l, k] = tile
                 remote(l, "fi", k, chip, fi_send.at[l, k], fi_recv.at[l, chip], "row", 2 * k + par).start()
+                remote(l, "fg", k, chip, fg_send.at[l, k], fg_recv.at[l, chip], "row", 2 * k + par).start()
             else:
                 f_own[...] = both
-        total = f_own[...]
+                fg_recv[l, k] = tile
+        wait_stats(l, "st2", 1, row_order[:-1])
+        pairs = [merge(stats(l, 1, 2 * k), stats(l, 1, 2 * k + 1)) for k in range(n_chip)]
+        coef = global_norm(pairs)
+        total = pick_slice(bf1, l, row * ffb, ffb)
+        for k in range(n_chip):
+            if k == 0:
+                scale_own, shift_own = coef[0]
+            else:
+                scale_own = jnp.where(chip == k, coef[k][0], scale_own)
+                shift_own = jnp.where(chip == k, coef[k][1], shift_own)
+
+        def add(total, k, part, scale, shift):
+            tile = fg_recv[l, k]
+            g = jnp.concatenate([tile[i:i + 1] for i in range(lanes)], axis=1)
+            b = jnp.concatenate([tile[lanes + i:lanes + i + 1] for i in range(lanes)], axis=1)
+            return total + (scale * part + (shift * g + b))
+
+        total = add(total, chip, f_own[...], scale_own, shift_own)
         for off in (1, 3, 2):
             k = lax.rem(chip + off, n_chip)
             remote(l, "fi", k, k, fi_send.at[l, k], fi_recv.at[l, k], "row", 2 * k + par).wait_recv()
-            total = total + fi_recv[l, k].astype(F32)
-        u = jnp.maximum((total + pick_slice(bf1, l, row * ffb, ffb)).astype(BF16), 0)
+            remote(l, "fg", k, k, fg_send.at[l, k], fg_recv.at[l, k], "row", 2 * k + par).wait_recv()
+            scale, shift = coef[0]
+            for i in range(1, n_chip):
+                scale = jnp.where(k == i, coef[i][0], scale)
+                shift = jnp.where(k == i, coef[i][1], shift)
+            total = add(total, k, fi_recv[l, k].astype(F32), scale, shift)
+        u = jnp.maximum(total.astype(BF16), 0)
 
         ug_recv[l, row] = u
         for off in offs[:-1]:
@@ -345,17 +358,16 @@
             done("wo", t, wo_recv.at[l, col], "col", j)
             done("fo", t, fo_recv.at[l, col], "col", j)
         for w in range(3):
-            done("qd", w, qd_send.at[l, w], "row", partner)
+            for j in row_order:
+                done("qi", w * n_row + j, qi_send.at[l, w, j], "row", j)
         pltpu.make_async_copy(k_stage.at[l], k_out.at[l], out_sem.at[l, 0]).wait()
         pltpu.make_async_copy(v_stage.at[l], v_out.at[l], out_sem.at[l, 1]).wait()
         for off in offs:
             k = lax.rem(chip + off, n_chip)
-            for w in range(3):
-                if off:
-                    done("qi", w * n_chip + k, qi_send.at[l, w, k], "row", 2 * k + par)
             done("fd", k, fd_send.at[l, k], "row", partner)
             if off:
                 done("fi", k, fi_send.at[l, k], "row", 2 * k + par)
+                done("fg", k, fg_send.at[l, k], "row", 2 * k + par)
                 done("ug", 2 * k + par, ug_recv.at[l, row], "row", 2 * k + par)
                 done("ug", 2 * k + 1 - par, ug_recv.at[l, 2 * k + par], "row", partner)
             else:
@@ -398,14 +410,13 @@
         scratch = local + [
             vm((batch, width)),
             vm((n_layer, 2, 8, 128), F32), vm((n_layer, 2, n_row, 8, 128), F32),
-            vm((n_layer, 3, batch + 16, n_chip * hd)), vm((n_layer, 3, batch + 16, n_chip * hd)),
-            vm((3, batch + 16, n_chip * hd), F32), vm((3, batch, hd), F32),
-            vm((n_layer, 3, n_chip, batch, hd)), vm((n_layer, 3, n_chip, batch, hd)),
+            vm((n_layer, 3, n_row, batch + 16, hd)), vm((n_layer, 3, n_row, batch + 16, hd)),
             vm((n_layer, batch, hd)), vm((n_layer, batch, hd)), vm((n_layer, n_row, batch, hd)),
             vm((n_layer, n_col, batch, width)),
             vm((n_layer, n_chip, batch + 16, ffb)), vm((n_layer, n_chip, batch + 16, ffb)),
             vm((n_chip, batch + 16, ffb), F32), vm((batch, ffb), F32),
             vm((n_layer, n_chip, batch, ffb)), vm((n_layer, n_chip, batch, ffb)),
+            vm((n_layer, n_chip, 2 * ffb // 128, 128), F32), vm((n_layer, n_chip, 2 * ffb // 128, 128), F32),
             vm((n_layer, n_row, batch, ffb)),
             vm((n_layer, n_col, batch, width)),
             pltpu.SemaphoreType.DMA((12,)), pltpu.SemaphoreType.DMA((n_layer, 8)), pltpu.SemaphoreType.DMA((n_layer, 3)),

time: 94.2 us -> 89 us (0.945)
  Pallas kernels: 89.1 us -> 83.8 us
    pallas_call x1, Pallas kernels: 89.1 us -> 83.8 us  [local_step(): pl.pallas_call(functools.partial(kernel, (n_layer, n_row, n_col, table)),...]
where the time goes in v3:
time: 89 us; the launch traced here: 88.7 us
  Pallas kernels  83.8 us (94%)
  local copies, waits for them, and re-layouts  4.22 us (5%)
    pallas_call x1, Pallas kernels, local_step(): pl.pallas_call(functools.partial(kernel, (n_layer, n_row, n_col, table)),...  83.8 us
    unnamed x3, local copies, waits for them, and re-layouts  4.22 us

profile of v3, /device:TPU:97, one launch (start us, length us, event | category | flops | bytes accessed | tf_op | source)
XLA Modules:
  0.0 88.7 jit_solution(13221469399376575777)
XLA Ops:
  0.6 83.8 %shard_map.211 = (bf16[64,512]{1,0:T(8,128)(2,1)}, bf16[2,64,128]{2,1,0:T(8,128)(2,1)}, bf16[2,64,128]{2,1,0:T(8,128)(2,1)}) custom-call(bf16[64,512]{1,0:T(8,128)(2,1)} %hid_hbm.1, s32[1,64]{1,0:T(1,128)} %bitcast.9, bf16[2,64,1,256,128]{4,3,2,1,0:T(8,128)(2,1)} %kc_hbm.1, bf16[2,64,1,256,128]{4,3,2,1,0:T(8,128)(2,1)} %vc_hbm.1, bf16[2,512]{1,0:T(2,128)(2,1)} %g1_hbm.1, ...), custom_call_target="tpu_custom_call" | custom-call | tf_op jit(solution)/shard_map/pallas_call | solution.py:428
  84.5 1.5 %copy.28 = bf16[64,512]{1,0:T(8,128)(2,1)} copy(bf16[64,512]{1,0:T(8,128)(2,1)} %get-tuple-element.15) | data formatting | bytes 131072
  86.0 1.4 %copy.29 = bf16[2,64,1,128]{3,1,2,0:T(8,128)(2,1)} copy(bf16[2,64,1,128]{3,1,2,0:T(8,128)(2,1)} %bitcast.8) | data formatting | bytes 65536
  87.3 1.4 %copy.30 = bf16[2,64,1,128]{3,1,2,0:T(8,128)(2,1)} copy(bf16[2,64,1,128]{3,1,2,0:T(8,128)(2,1)} %bitcast.7) | data formatting | bytes 65536

commit v4 on v3

v4 whole, which is shorter than its diff:
```python
import functools

import jax
import jax.numpy as jnp
from jax import lax
from jax.experimental import pallas as pl
from jax.experimental.pallas import tpu as pltpu
from jax.sharding import PartitionSpec as P

EPS_LN = 1e-5
VLIM = 66 * 1000 * 1000
MESH = pl.DeviceIdType.MESH
F32 = jnp.float32
BF16 = jnp.bfloat16


class Sems:
    def __init__(self):
        self.count = 0

    def take(self, n):
        base = self.count
        self.count += n
        return base


def layout():
    sems = Sems()
    names = dict(st1=1, st1p=1, st2=1, st2p=1, q=1, kd=1, vd=1, k=1, v=1, ag=1, wo=1, fd=4, fi=1, fg=1, ug=8, fo=1)
    table = {name: sems.take(n) for name, n in names.items()}
    return table, sems.count


def kernel(dims, hid_hbm, len_hbm, kc_hbm, vc_hbm, g1_hbm, b1_hbm, wq_hbm, bq_hbm, wk_hbm, bk_hbm, wv_hbm, bv_hbm,
           wo_hbm, bo_hbm, g2_hbm, b2_hbm, w1_hbm, bf1_hbm, w2_hbm, bf2_hbm,
           h_out, k_out, v_out,
           hid_v, len_v, kc, vc, g1, b1, wq, bq, wk, bk, wv, bv, wo, bo, g2, b2, w1, bf1, w2, bf2,
           state, st_send, st_recv, q_send, q_recv, kd_send, kd_recv, k_mine, k_send, k_recv, k_stage, v_stage,
           ag_recv, wo_recv, fd_send, fd_recv, f_mine, f_own, fi_send, fi_recv, fg_send, fg_recv, ug_recv, fo_recv,
           small_sem, big_sem, out_sem, ssem, rsem):
    n_layer, n_row, n_col, table = dims
    n_chip = n_row // 2
    row = lax.axis_index("row")
    col = lax.axis_index("col")
    chip = row // 2
    par = row % 2
    partner = row + 1 - 2 * par
    batch, width = hid_v.shape
    hd = kc.shape[-1]
    keys = kc.shape[2]
    ffb = fd_send.shape[-1]
    offs = [2, 1, 3, 0]
    chips = {off: lax.rem(chip + off, n_chip) for off in offs}
    row_order = []
    for off in offs[:-1]:
        row_order += [2 * chips[off] + par, 2 * chips[off] + 1 - par]

    barrier = pltpu.get_barrier_semaphore()
    for t in range(1, n_row):
        pl.semaphore_signal(barrier, inc=1, device_id={"row": lax.rem(row + t, n_row)}, device_id_type=MESH)
    for t in range(1, n_col):
        pl.semaphore_signal(barrier, inc=1, device_id={"col": lax.rem(col + t, n_col)}, device_id_type=MESH)

    small = [(hid_hbm, hid_v), (len_hbm, len_v), (g1_hbm, g1), (b1_hbm, b1), (bq_hbm, bq), (bk_hbm, bk),
             (bv_hbm, bv), (bo_hbm, bo), (g2_hbm, g2), (b2_hbm, b2), (bf1_hbm, bf1), (bf2_hbm, bf2)]
    small_copies = [pltpu.make_async_copy(s, d, small_sem.at[i]) for i, (s, d) in enumerate(small)]
    for c in small_copies:
        c.start()

    bigs = [(wq_hbm, wq), (wk_hbm, wk), (wv_hbm, wv), (kc_hbm, kc), (vc_hbm, vc), (wo_hbm, wo), (w1_hbm, w1),
            (w2_hbm, w2)]
    WQ, WK, WV, KC, VC, WO, W1, W2 = range(8)

    def big_copy(i, l):
        s, d = bigs[i]
        src = s.at[l, :, 0] if i in (KC, VC) else s.at[l]
        return pltpu.make_async_copy(src, d.at[l], big_sem.at[l, i])

    for i in (WQ, WK, WV):
        big_copy(i, 0).start()

    small_copies[0].wait()
    state[...] = hid_v[...]

    def enter():
        pl.semaphore_wait(barrier, n_row - 1 + n_col - 1)

    def rest_of_loads():
        for i in (KC, VC, WO, W1, W2):
            big_copy(i, 0).start()
        for l in range(1, n_layer):
            for i in range(8):
                big_copy(i, l).start()
        for c in small_copies[1:]:
            c.wait()

    def remote(name, i, src, dst, axis, target):
        sem = table[name] + i
        return pltpu.make_async_remote_copy(src_ref=src, dst_ref=dst, send_sem=ssem.at[sem], recv_sem=rsem.at[sem],
                                            device_id={axis: target}, device_id_type=MESH)

    def got(name, i, ref, axis="row"):
        remote(name, i, ref, ref, axis, partner if axis == "row" else lax.rem(col + 1, n_col)).wait_recv()

    def sent(name, i, ref, axis="row"):
        remote(name, i, ref, ref, axis, partner if axis == "row" else lax.rem(col + 1, n_col)).wait_send()

    def pick(ref, l):
        rows = ref[...].astype(F32)
        out = rows[0:1]
        for i in range(1, n_layer):
            out = jnp.where(l == i, rows[i:i + 1], out)
        return out

    def pick_slice(ref, l, start, size):
        rows = ref[:, pl.ds(pl.multiple_of(start, size), size)].astype(F32)
        out = rows[0:1]
        for i in range(1, n_layer):
            out = jnp.where(l == i, rows[i:i + 1], out)
        return out

    eye = lax.broadcasted_iota(jnp.int32, (batch, 128), 0) == lax.broadcasted_iota(jnp.int32, (batch, 128), 1)

    def to_row(column):
        return jnp.sum(jnp.where(eye, column, 0.0), axis=0, keepdims=True)

    def to_column(line):
        return jnp.sum(jnp.where(eye, line, 0.0), axis=1, keepdims=True)

    def local_norm(l, name, which, gain, shift):
        x = state[...].astype(F32)
        c = jnp.sum(x, axis=1, keepdims=True) / width
        xc = x - c
        v = jnp.sum(xc * xc, axis=1, keepdims=True) / width
        sub = lax.broadcasted_iota(jnp.int32, (8, 128), 0)
        tile = jnp.where(sub == 0, to_row(c), jnp.where(sub == 1, to_row(v), 0.0))
        st_send[l, which] = tile
        if which == 0:
            pl.when(l == 0)(enter)
        for j in row_order:
            remote(name, 0, st_send.at[l, which], st_recv.at[l, which, row], "row", j).start()
        remote(name + "p", 0, st_send.at[l, which], st_recv.at[l, which, row], "row", partner).start()
        st_recv[l, which, row] = tile
        if which == 0:
            pl.when(l == 0)(rest_of_loads)
        g, b = pick(gain, l), pick(shift, l)
        y = xc * lax.rsqrt(v + EPS_LN) * g
        extra = lax.broadcasted_iota(jnp.int32, (16, 1), 0)
        extra = jnp.where(extra == 0, g, jnp.where(extra == 1, b, 0.0))
        return jnp.concatenate([y.astype(BF16), extra.astype(BF16)], axis=0)

    def scale_of(v):
        return (v + EPS_LN) * lax.rsqrt(v + EPS_LN)

    def global_norm(parts):
        m = sum(c for c, _ in parts) / len(parts)
        var = sum(v + (c - m) * (c - m) for c, v in parts) / len(parts)
        r = lax.rsqrt(var + EPS_LN)
        return [(to_column(r * scale_of(v)), to_column(r * (c - m))) for c, v in parts]

    def stats(l, which, j):
        tile = st_recv[l, which, j]
        return tile[0:1], tile[1:2]

    def merge(one, two):
        half = 0.5 * (one[0] - two[0])
        return 0.5 * (one[0] + two[0]), 0.5 * (one[1] + two[1]) + half * half

    def pair_merge(l, which):
        here, there = stats(l, which, row), stats(l, which, partner)
        c_pair, v_pair = merge(here, there)
        r_pair = lax.rsqrt(v_pair + EPS_LN)
        a_own, a_got = to_column(r_pair * scale_of(here[1])), to_column(r_pair * scale_of(there[1]))
        d_own = to_column(r_pair * (here[0] - c_pair))

        def rows(own, got_rows):
            return ((a_own * own[:batch] + a_got * got_rows[:batch])
                    + d_own * (own[batch:batch + 1] - got_rows[batch:batch + 1]))

        return rows

    def pair_coefficients(l, which):
        return global_norm([merge(stats(l, which, 2 * k), stats(l, which, 2 * k + 1)) for k in range(n_chip)])

    def ar_col(l, name, part, buf, bias):
        buf[l, col] = part.astype(BF16)
        for t in (2, 1, 3):
            remote(name, 0, buf.at[l, col], buf.at[l, col], "col", lax.rem(col + t, n_col)).start()
        if name == "fo":
            drain(l)
        got(name, 0, buf.at[l, pl.ds(0, n_col - 1)], "col")
        total = buf[l, 0].astype(F32)
        for j in range(1, n_col):
            total = total + buf[l, j].astype(F32)
        state[...] = (state[...].astype(F32) + (total + bias)).astype(BF16)
        sent(name, 0, buf.at[l, pl.ds(0, n_col - 1)], "col")

    def drain(l):
        for which, name in ((0, "st1"), (1, "st2")):
            sent(name, 0, st_recv.at[l, which, pl.ds(0, n_row - 2)])
            sent(name + "p", 0, st_recv.at[l, which, 0])
        sent("q", 0, q_recv.at[l, pl.ds(0, n_row - 1)])
        for w, (d, i) in enumerate((("kd", "k"), ("vd", "v"))):
            sent(d, 0, kd_send.at[l, w])
            sent(i, 0, k_send.at[l, w, pl.ds(0, n_chip - 1)])
        sent("ag", 0, ag_recv.at[l, pl.ds(0, n_row - 1)])
        for k in range(n_chip):
            sent("fd", k, fd_send.at[l, k])
        sent("fi", 0, fi_send.at[l, pl.ds(0, n_chip - 1)])
        sent("fg", 0, fg_send.at[l, pl.ds(0, n_chip - 1)])
        for j in range(n_row - 1):
            sent("ug", j, ug_recv.at[l, j])

    def layer(l, carry):
        y = local_norm(l, "st1", 0, g1, b1)

        big_copy(WQ, l).wait()
        res = jnp.dot(y, wq[l], preferred_element_type=F32).astype(BF16)
        for j in range(n_row):
            q_send[l, j] = res[:, j * hd:(j + 1) * hd]
        for j in row_order + [partner]:
            remote("q", 0, q_send.at[l, j], q_recv.at[l, row], "row", j).start()
        q_recv[l, row] = q_send[l, row]

        for i_big, w_ref in ((WK, wk), (WV, wv)):
            big_copy(i_big, l).wait()
        for w, (name, w_ref) in enumerate((("kd", wk), ("vd", wv))):
            res = jnp.dot(y, w_ref[l], preferred_element_type=F32)
            even = jnp.concatenate([res[:, 2 * k * hd:(2 * k + 1) * hd] for k in range(n_chip)], axis=1)
            odd = jnp.concatenate([res[:, (2 * k + 1) * hd:(2 * k + 2) * hd] for k in range(n_chip)], axis=1)
            kd_send[l, w] = jnp.where(par == 0, odd, even).astype(BF16)
            remote(name, 0, kd_send.at[l, w], kd_recv.at[l, w], "row", partner).start()
            k_mine[w] = jnp.where(par == 0, even, odd)

        got("st1p", 0, st_recv.at[l, 0, 0])
        merged = pair_merge(l, 0)
        for w, (d_name, name) in enumerate((("kd", "k"), ("vd", "v"))):
            got(d_name, 0, kd_recv.at[l, w])
            own, other = k_mine[w], kd_recv[l, w].astype(F32)
            both = jnp.concatenate([merged(own, other), own[batch:] + other[batch:]], axis=0).astype(BF16)
            for k in range(n_chip):
                k_send[l, w, k] = both[:, k * hd:(k + 1) * hd]
            for off in offs[:-1]:
                k = chips[off]
                remote(name, 0, k_send.at[l, w, k], k_recv.at[l, w, chip], "row", 2 * k + par).start()
            k_recv[l, w, chip] = k_send[l, w, chip]

        def collect(parts, coefs, bias):
            total = pick_slice(bias, l, row * hd, hd)
            for part, (scale, shift) in zip(parts, coefs):
                part = part.astype(F32)
                total = total + (scale * part[:batch] + (shift * part[batch:batch + 1] + part[batch + 1:batch + 2]))
            return total

        got("st1", 0, st_recv.at[l, 0, pl.ds(0, n_row - 2)])
        coef = global_norm([stats(l, 0, j) for j in range(n_row)])
        coef_pair = pair_coefficients(l, 0)
        got("q", 0, q_recv.at[l, pl.ds(0, n_row - 1)])
        q = collect([q_recv[l, j] for j in range(n_row)], coef, bq)
        q = (q * (hd ** -0.5)).astype(BF16).astype(F32)

        group = 16
        rowi = lax.broadcasted_iota(jnp.int32, (group, 1), 0)
        big_copy(KC, l).wait()
        parts = []
        for g in range(batch // group):
            q_g = q[g * group:(g + 1) * group]
            lhs = jnp.concatenate([jnp.where(rowi == i, q_g, 0.0) for i in range(group)], axis=1).astype(BF16)
            k_g = jnp.concatenate([kc[l, g * group + i] for i in range(group)], axis=1)
            parts.append(lax.dot_general(lhs, k_g, (((1,), (1,)), ((), ())), preferred_element_type=F32))
        scores = jnp.concatenate(parts, axis=0)
        lens = jnp.sum(jnp.where(eye, jnp.pad(len_v[...], ((0, 0), (0, 128 - batch))), 0), axis=1, keepdims=True)
        scores = jnp.where(lax.broadcasted_iota(jnp.int32, (batch, keys), 1) < lens, scores, -jnp.inf)
        got("k", 0, k_recv.at[l, 0, pl.ds(0, n_chip - 1)])
        k_new = collect([k_recv[l, 0, k] for k in range(n_chip)], coef_pair, bk).astype(BF16)
        k_stage[l] = k_new
        pltpu.make_async_copy(k_stage.at[l], k_out.at[l], out_sem.at[l, 0]).start()
        s_new = jnp.sum(q * k_new.astype(F32), axis=1, keepdims=True)
        peak = jnp.maximum(jnp.max(scores, axis=1, keepdims=True), s_new)
        e = jnp.exp(scores - peak)
        e_new = jnp.exp(s_new - peak)
        mass = jnp.sum(e, axis=1, keepdims=True) + e_new
        prob = (e / mass).astype(BF16).astype(F32)
        prob_new = (e_new / mass).astype(BF16).astype(F32)
        big_copy(VC, l).wait()
        outs = []
        for g in range(batch // group):
            p_g = prob[g * group:(g + 1) * group]
            lhs = jnp.concatenate([jnp.where(rowi // 2 == i, p_g, 0.0) for i in range(group // 2)],
                                  axis=1).astype(BF16)
            v_g = jnp.concatenate([jnp.concatenate([vc[l, g * group + 2 * i], vc[l, g * group + 2 * i + 1]], axis=1)
                                   for i in range(group // 2)], axis=0)
            out = jnp.dot(lhs, v_g, preferred_element_type=F32)
            outs.append(jnp.where(rowi % 2 == 0, out[:, :hd], out[:, hd:]))
        got("v", 0, k_recv.at[l, 1, pl.ds(0, n_chip - 1)])
        v_new = collect([k_recv[l, 1, k] for k in range(n_chip)], coef_pair, bv).astype(BF16)
        mixed = jnp.concatenate(outs, axis=0) + prob_new * v_new.astype(F32)

        ag_recv[l, row] = mixed.astype(BF16)
        for j in row_order + [partner]:
            remote("ag", 0, ag_recv.at[l, row], ag_recv.at[l, row], "row", j).start()
        v_stage[l] = v_new
        pltpu.make_async_copy(v_stage.at[l], v_out.at[l], out_sem.at[l, 1]).start()
        big_copy(WO, l).wait()
        got("ag", 0, ag_recv.at[l, pl.ds(0, n_row - 1)])
        gathered = jnp.concatenate([ag_recv[l, j] for j in range(n_row)], axis=1)
        ar_col(l, "wo", jnp.dot(gathered, wo[l], preferred_element_type=F32), wo_recv, pick(bo, l))

        y2 = local_norm(l, "st2", 1, g2, b2)
        big_copy(W1, l).wait()

        def fc1_block(j):
            return jnp.dot(y2, w1[l, :, pl.ds(pl.multiple_of(j * ffb, ffb), ffb)], preferred_element_type=F32)

        for some in (offs[:2], offs[2:]):
            blocks = [fc1_block(2 * chips[off] + 1 - par).astype(BF16) for off in some]
            for off, block in zip(some, blocks):
                fd_send[l, chips[off]] = block
            for off in some:
                k = chips[off]
                remote("fd", k, fd_send.at[l, k], fd_recv.at[l, k], "row", partner).start()
        blocks = [fc1_block(2 * chips[off] + par) for off in offs]
        for off, block in zip(offs, blocks):
            f_mine[chips[off]] = block
        got("st2p", 0, st_recv.at[l, 1, 0])
        merged = pair_merge(l, 1)
        lanes = ffb // 128
        for off in offs:
            k = chips[off]
            got("fd", k, fd_recv.at[l, k])
            own, other = f_mine[k], fd_recv[l, k].astype(F32)
            both = merged(own, other)
            gb = own[batch:] + other[batch:]
            gb = jnp.concatenate([gb[0:1], gb[1:2]], axis=1)
            tile = jnp.concatenate([gb[:, i * 128:(i + 1) * 128] for i in range(2 * lanes)], axis=0)
            if off:
                fi_send[l, k] = both.astype(BF16)
                fg_send[l, k] = tile
                remote("fi", 0, fi_send.at[l, k], fi_recv.at[l, chip], "row", 2 * k + par).start()
                remote("fg", 0, fg_send.at[l, k], fg_recv.at[l, chip], "row", 2 * k + par).start()
            else:
                fi_recv[l, k] = both.astype(BF16)
                fg_recv[l, k] = tile
        got("st2", 0, st_recv.at[l, 1, pl.ds(0, n_row - 2)])
        coef = pair_coefficients(l, 1)
        total = pick_slice(bf1, l, row * ffb, ffb)
        got("fg", 0, fg_recv.at[l, pl.ds(0, n_chip - 1)])
        got("fi", 0, fi_recv.at[l, pl.ds(0, n_chip - 1)])
        for k in range(n_chip):
            tile = fg_recv[l, k]
            g = jnp.concatenate([tile[i:i + 1] for i in range(lanes)], axis=1)
            b = jnp.concatenate([tile[lanes + i:lanes + i + 1] for i in range(lanes)], axis=1)
            total = total + (coef[k][0] * fi_recv[l, k].astype(F32) + (coef[k][1] * g + b))
        u = jnp.maximum(total.astype(BF16), 0)

        ug_recv[l, row] = u
        for off in offs[:-1]:
            remote("ug", n_chip - off, ug_recv.at[l, row], ug_recv.at[l, row], "row", 2 * chips[off] + par).start()
        remote("ug", 0, ug_recv.at[l, row], ug_recv.at[l, row], "row", partner).start()
        big_copy(W2, l).wait()

        def fc2_block(j):
            return jnp.dot(ug_recv[l, j], w2[l, pl.ds(pl.multiple_of(j * ffb, ffb), ffb), :],
                           preferred_element_type=F32)

        acc = jnp.dot(u, w2[l, pl.ds(pl.multiple_of(row * ffb, ffb), ffb), :], preferred_element_type=F32)
        got("ug", 0, ug_recv.at[l, partner])
        acc = acc + fc2_block(partner)

        def same(off):
            return 2 * chips[off] + par

        def cross(off):
            return 2 * chips[off] + 1 - par

        def pass_on(off):
            got("ug", off, ug_recv.at[l, same(off)])
            remote("ug", n_chip - 1 + off, ug_recv.at[l, same(off)], ug_recv.at[l, same(off)], "row", partner).start()

        pass_on(1)
        pass_on(3)
        acc = acc + (fc2_block(same(1)) + fc2_block(same(3)))
        pass_on(2)
        got("ug", n_chip, ug_recv.at[l, cross(1)])
        got("ug", n_chip + 2, ug_recv.at[l, cross(3)])
        acc = acc + (fc2_block(same(2)) + fc2_block(cross(1)) + fc2_block(cross(3)))
        got("ug", n_chip + 1, ug_recv.at[l, cross(2)])
        ar_col(l, "fo", acc + fc2_block(cross(2)), fo_recv, pick(bf2, l))
        return carry

    lax.fori_loop(0, n_layer, layer, 0)
    pltpu.make_async_copy(state, h_out, out_sem.at[0, 2]).start()
    for l in range(n_layer):
        pltpu.make_async_copy(k_stage.at[l], k_out.at[l], out_sem.at[l, 0]).wait()
        pltpu.make_async_copy(v_stage.at[l], v_out.at[l], out_sem.at[l, 1]).wait()
    pltpu.make_async_copy(state, h_out, out_sem.at[0, 2]).wait()


def finish(h, k, v, h_out, k_out, v_out, h_v, k_v, v_v, sem_in, sem_out):
    loads = [pltpu.make_async_copy(s, d, sem_in.at[i]) for i, (s, d) in enumerate(((h, h_v), (k, k_v), (v, v_v)))]
    stores = [pltpu.make_async_copy(s, d, sem_out.at[i])
              for i, (s, d) in enumerate(((h_v, h_out), (k_v, k_out), (v_v, v_out)))]
    for c in loads:
        c.start()
    for c, d in zip(loads, stores):
        c.wait()
        d.start()
    for d in stores:
        d.wait()


def solution(mesh):
    n_row, n_col = mesh.shape["row"], mesh.shape["col"]
    n_chip = n_row // 2
    act_spec = P("dp", "row")
    cache_spec = P(None, "dp", ("col", "row"), None, None)
    fresh_spec = P(None, "dp", ("col", "row"), None)
    in_weight = P(None, "row", "col")
    out_weight = P(None, "col", "row")
    col_vec = P(None, "col")
    row_vec = P(None, "row")
    in_specs = (act_spec, P("dp"), cache_spec, cache_spec, row_vec, row_vec,
                in_weight, col_vec, in_weight, col_vec, in_weight, col_vec,
                out_weight, row_vec, row_vec, row_vec, in_weight, col_vec, out_weight, row_vec)

    def local_step(hidden, cache_len, k_cache, v_cache, ln1_g, ln1_b, w_q, b_q, w_k, b_k, w_v, b_v,
                   w_o, b_o, ln2_g, ln2_b, w_fc1, b_fc1, w_fc2, b_fc2):
        batch, width = hidden.shape
        n_layer, _, _, keys, hd = k_cache.shape
        ff = w_fc1.shape[2]
        ffb = ff // n_row
        table, n_sem = layout()
        args = (hidden, cache_len.reshape(1, batch), k_cache, v_cache, ln1_g, ln1_b, w_q, b_q, w_k, b_k, w_v, b_v,
                w_o, b_o, ln2_g, ln2_b, w_fc1, b_fc1, w_fc2, b_fc2)

        def vm(shape, dtype=BF16):
            return pltpu.VMEM(shape, dtype)

        local = [vm(a.shape, a.dtype) for a in args]
        local[2] = local[3] = vm((n_layer, batch, keys, hd))
        scratch = local + [
            vm((batch, width)),
            vm((n_layer, 2, 8, 128), F32), vm((n_layer, 2, n_row, 8, 128), F32),
            vm((n_layer, n_row, batch + 16, hd)), vm((n_layer, n_row, batch + 16, hd)),
            vm((n_layer, 2, batch + 16, n_chip * hd)), vm((n_layer, 2, batch + 16, n_chip * hd)),
            vm((2, batch + 16, n_chip * hd), F32),
            vm((n_layer, 2, n_chip, batch + 16, hd)), vm((n_layer, 2, n_chip, batch + 16, hd)),
            vm((n_layer, batch, hd)), vm((n_layer, batch, hd)),
            vm((n_layer, n_row, batch, hd)), vm((n_layer, n_col, batch, width)),
            vm((n_layer, n_chip, batch + 16, ffb)), vm((n_layer, n_chip, batch + 16, ffb)),
            vm((n_chip, batch + 16, ffb), F32), vm((batch, ffb), F32),
            vm((n_layer, n_chip, batch, ffb)), vm((n_layer, n_chip, batch, ffb)),
            vm((n_layer, n_chip, 2 * ffb // 128, 128), F32), vm((n_layer, n_chip, 2 * ffb // 128, 128), F32),
            vm((n_layer, n_row, batch, ffb)), vm((n_layer, n_col, batch, width)),
            pltpu.SemaphoreType.DMA((12,)), pltpu.SemaphoreType.DMA((n_layer, 8)), pltpu.SemaphoreType.DMA((n_layer, 3)),
            pltpu.SemaphoreType.DMA((n_sem,)), pltpu.SemaphoreType.DMA((n_sem,)),
        ]
        out_shape = (jax.ShapeDtypeStruct((batch, width), BF16),
                     jax.ShapeDtypeStruct((n_layer, batch, hd), BF16),
                     jax.ShapeDtypeStruct((n_layer, batch, hd), BF16))
        h_out, k_new, v_new = pl.pallas_call(
            functools.partial(kernel, (n_layer, n_row, n_col, table)),
            out_shape=out_shape,
            in_specs=[pl.BlockSpec(memory_space=pl.ANY)] * len(args),
            out_specs=[pl.BlockSpec(memory_space=pl.ANY)] * 3,
            scratch_shapes=scratch,
            compiler_params=pltpu.CompilerParams(collective_id=0, has_side_effects=True,
                                                 vmem_limit_bytes=VLIM),
        )(*args)
        h_out, k_new, v_new = pl.pallas_call(
            finish, out_shape=out_shape,
            in_specs=[pl.BlockSpec(memory_space=pl.ANY)] * 3, out_specs=[pl.BlockSpec(memory_space=pl.ANY)] * 3,
            scratch_shapes=[vm(o.shape) for o in out_shape] + [pltpu.SemaphoreType.DMA((3,))] * 2,
        )(h_out, k_new, v_new)
        return h_out, k_new[:, :, None, :], v_new[:, :, None, :]

    return jax.shard_map(local_step, mesh=mesh, in_specs=in_specs,
                         out_specs=(act_spec, fresh_spec, fresh_spec), check_vma=False)
```

time: 89 us -> 82.2 us (0.924)
  local copies, waits for them, and re-layouts: 4.22 us -> 0 us
  Pallas kernels: 83.8 us -> 81.4 us
    unnamed x3 -> x0, local copies, waits for them, and re-layouts: 4.22 us -> none
    pallas_call x1, Pallas kernels: 83.8 us -> 79.9 us  [local_step(): pl.pallas_call(functools.partial(kernel, (n_layer, n_row, n_col, table)),...]
    pallas_call x0 -> x1, Pallas kernels: none -> 1.54 us  [local_step(): pl.pallas_call(finish, out_shape=out_shape, in_specs=[pl.BlockSpec(memory...]
where the time goes in v4:
time: 82.2 us; the launch traced here: 82.1 us
  Pallas kernels  81.4 us (99%)
    pallas_call x1, Pallas kernels, local_step(): pl.pallas_call(functools.partial(kernel, (n_layer, n_row, n_col, table)),...  79.9 us

profile of v4, /device:TPU:97, one launch (start us, length us, event | category | flops | bytes accessed | tf_op | source)
XLA Modules:
  0.0 82.1 jit_solution(7701551154354997115)
XLA Ops:
  0.6 79.9 %shard_map.211 = (bf16[64,512]{1,0:T(8,128)(2,1)}, bf16[2,64,128]{2,1,0:T(8,128)(2,1)}, bf16[2,64,128]{2,1,0:T(8,128)(2,1)}) custom-call(bf16[64,512]{1,0:T(8,128)(2,1)} %hid_hbm.1, s32[1,64]{1,0:T(1,128)} %bitcast.7, bf16[2,64,1,256,128]{4,3,2,1,0:T(8,128)(2,1)} %kc_hbm.1, bf16[2,64,1,256,128]{4,3,2,1,0:T(8,128)(2,1)} %vc_hbm.1, bf16[2,512]{1,0:T(2,128)(2,1)} %g1_hbm.1, ...), custom_call_target="tpu_custom_call" | custom-call | tf_op jit(solution)/shard_map/pallas_call | solution.py:461
  80.5 1.5 %shard_map.212 = (bf16[64,512]{1,0:T(8,128)(2,1)}, bf16[2,64,128]{2,1,0:T(8,128)(2,1)}, bf16[2,64,128]{2,1,0:T(8,128)(2,1)}) custom-call(bf16[64,512]{1,0:T(8,128)(2,1)} %get-tuple-element.9.h, bf16[2,64,128]{2,1,0:T(8,128)(2,1)} %get-tuple-element.10.k, bf16[2,64,128]{2,1,0:T(8,128)(2,1)} %get-tuple-element.11.v), custom_call_target="tpu_custom_call" | custom-call | tf_op jit(solution)/shard_map/pallas_call | solution.py:470

commit v5 on v4

v5 whole, which is shorter than its diff:
```python
import functools

import jax
import jax.numpy as jnp
from jax import lax
from jax.experimental import pallas as pl
from jax.experimental.pallas import tpu as pltpu
from jax.sharding import PartitionSpec as P

EPS_LN = 1e-5
VLIM = 66 * 1000 * 1000
MESH = pl.DeviceIdType.MESH
F32 = jnp.float32
BF16 = jnp.bfloat16


class Sems:
    def __init__(self):
        self.count = 0

    def take(self, n):
        base = self.count
        self.count += n
        return base


HALVES = 2


def layout(n_chip):
    sems = Sems()
    names = dict(st1=1, st1p=1, st2=1, st2p=1, q=1, kd=1, vd=1, k=1, v=1, ag=1, wo=1, fd=n_chip, fi=1, fg=1,
                 ug=2 * n_chip - 1, fo=1)
    table = [{name: sems.take(n) for name, n in names.items()} for _ in range(HALVES)]
    return table, sems.count


def kernel(dims, hid_hbm, len_hbm, kc_hbm, vc_hbm, g1_hbm, b1_hbm, wq_hbm, bq_hbm, wk_hbm, bk_hbm, wv_hbm, bv_hbm,
           wo_hbm, bo_hbm, g2_hbm, b2_hbm, w1_hbm, bf1_hbm, w2_hbm, bf2_hbm,
           h_out, k_out, v_out, local, halves, state, sem):
    n_layer, n_row, n_col, table = dims
    hid_v, len_v, kc, vc, g1, b1, wq, bq, wk, bk, wv, bv, wo, bo, g2, b2, w1, bf1, w2, bf2 = local
    small_sem, big_sem, out_sem, ssem, rsem = sem
    n_chip = n_row // 2
    row = lax.axis_index("row")
    col = lax.axis_index("col")
    chip = row // 2
    par = row % 2
    partner = row + 1 - 2 * par
    batch, width = hid_v.shape
    part = batch // HALVES
    hd = kc.shape[-1]
    keys = kc.shape[2]
    ffb = w1.shape[-1] // n_row
    lanes = ffb // 128
    offs = [2, 1, 3, 0]
    chips = {off: lax.rem(chip + off, n_chip) for off in offs}
    row_order = []
    for off in offs[:-1]:
        row_order += [2 * chips[off] + par, 2 * chips[off] + 1 - par]

    barrier = pltpu.get_barrier_semaphore()
    for t in range(1, n_row):
        pl.semaphore_signal(barrier, inc=1, device_id={"row": lax.rem(row + t, n_row)}, device_id_type=MESH)
    for t in range(1, n_col):
        pl.semaphore_signal(barrier, inc=1, device_id={"col": lax.rem(col + t, n_col)}, device_id_type=MESH)

    small = [(hid_hbm, hid_v), (g1_hbm, g1), (b1_hbm, b1), (len_hbm, len_v), (bq_hbm, bq), (bk_hbm, bk),
             (bv_hbm, bv), (bo_hbm, bo), (g2_hbm, g2), (b2_hbm, b2), (bf1_hbm, bf1), (bf2_hbm, bf2)]
    small_copies = [pltpu.make_async_copy(s, d, small_sem.at[i]) for i, (s, d) in enumerate(small)]
    bigs = [(wq_hbm, wq), (wk_hbm, wk), (wv_hbm, wv), (kc_hbm, kc), (vc_hbm, vc), (wo_hbm, wo), (w1_hbm, w1),
            (w2_hbm, w2)]
    WQ, WK, WV, KC, VC, WO, W1, W2 = range(8)

    def big_copy(i, l):
        s, d = bigs[i]
        src = s.at[l, :, 0] if i in (KC, VC) else s.at[l]
        return pltpu.make_async_copy(src, d.at[l], big_sem.at[l, i])

    for c in small_copies:
        c.start()
    for i in (WQ, WK, WV):
        big_copy(i, 0).start()
    small_copies[0].wait()
    state[...] = hid_v[...]

    def enter():
        pl.semaphore_wait(barrier, n_row - 1 + n_col - 1)

    def rest_of_small():
        for c in small_copies[1:]:
            c.wait()

    def rest_of_bulk():
        for i in (KC, VC, WO, W1, W2):
            big_copy(i, 0).start()
        for l in range(1, n_layer):
            for i in range(8):
                big_copy(i, l).start()

    def remote(h, name, i, src, dst, axis, target):
        at = table[h][name] + i
        return pltpu.make_async_remote_copy(src_ref=src, dst_ref=dst, send_sem=ssem.at[at], recv_sem=rsem.at[at],
                                            device_id={axis: target}, device_id_type=MESH)

    def same_bytes(h, name, i, ref, axis):
        return remote(h, name, i, ref, ref, axis, partner if axis == "row" else lax.rem(col + 1, n_col))

    def got(h, name, i, ref, axis="row"):
        same_bytes(h, name, i, ref, axis).wait_recv()

    def sent(h, name, i, ref, axis="row"):
        same_bytes(h, name, i, ref, axis).wait_send()

    def pick(ref, l):
        rows = ref[...].astype(F32)
        out = rows[0:1]
        for i in range(1, n_layer):
            out = jnp.where(l == i, rows[i:i + 1], out)
        return out

    def pick_slice(ref, l, start, size):
        rows = ref[:, pl.ds(pl.multiple_of(start, size), size)].astype(F32)
        out = rows[0:1]
        for i in range(1, n_layer):
            out = jnp.where(l == i, rows[i:i + 1], out)
        return out

    eye = lax.broadcasted_iota(jnp.int32, (part, 128), 0) == lax.broadcasted_iota(jnp.int32, (part, 128), 1)

    def to_row(column):
        return jnp.sum(jnp.where(eye, column, 0.0), axis=0, keepdims=True)

    def to_column(line):
        return jnp.sum(jnp.where(eye, line, 0.0), axis=1, keepdims=True)

    def local_norm(l, h, name, which, gain, shift):
        st_send, st_recv = halves[h]["st_send"], halves[h]["st_recv"]
        x = state[h * part:(h + 1) * part].astype(F32)
        c = jnp.sum(x, axis=1, keepdims=True) / width
        xc = x - c
        v = jnp.sum(xc * xc, axis=1, keepdims=True) / width
        sub = lax.broadcasted_iota(jnp.int32, (8, 128), 0)
        tile = jnp.where(sub == 0, to_row(c), jnp.where(sub == 1, to_row(v), 0.0))
        st_send[l, which] = tile
        if which == 0 and h == 0:
            pl.when(l == 0)(enter)
        for j in row_order:
            remote(h, name, 0, st_send.at[l, which], st_recv.at[l, which, row], "row", j).start()
        remote(h, name + "p", 0, st_send.at[l, which], st_recv.at[l, which, row], "row", partner).start()
        st_recv[l, which, row] = tile
        if which == 0 and h == 0:
            pl.when(l == 0)(rest_of_small)
        g, b = pick(gain, l), pick(shift, l)
        y = (xc * lax.rsqrt(v + EPS_LN) * g).astype(BF16)
        if h:
            return y
        extra = lax.broadcasted_iota(jnp.int32, (16, 1), 0)
        extra = jnp.where(extra == 0, g, jnp.where(extra == 1, b, 0.0))
        return jnp.concatenate([y, extra.astype(BF16)], axis=0)

    def scale_of(v):
        return (v + EPS_LN) * lax.rsqrt(v + EPS_LN)

    def global_norm(parts):
        m = sum(c for c, _ in parts) / len(parts)
        var = sum(v + (c - m) * (c - m) for c, v in parts) / len(parts)
        r = lax.rsqrt(var + EPS_LN)
        return [(to_column(r * scale_of(v)), to_column(r * (c - m))) for c, v in parts]

    def stats(l, h, which, j):
        tile = halves[h]["st_recv"][l, which, j]
        return tile[0:1], tile[1:2]

    def merge(one, two):
        half = 0.5 * (one[0] - two[0])
        return 0.5 * (one[0] + two[0]), 0.5 * (one[1] + two[1]) + half * half

    def pair_merge(l, h, which):
        here, there = stats(l, h, which, row), stats(l, h, which, partner)
        c_pair, v_pair = merge(here, there)
        r_pair = lax.rsqrt(v_pair + EPS_LN)
        a_own, a_got = to_column(r_pair * scale_of(here[1])), to_column(r_pair * scale_of(there[1]))
        d_own = to_column(r_pair * (here[0] - c_pair))

        def rows(own, other, g_own, g_other):
            return (a_own * own[:part] + a_got * other[:part]) + d_own * (g_own - g_other)

        return rows

    def pair_coefficients(l, h, which):
        return global_norm([merge(stats(l, h, which, 2 * k), stats(l, h, which, 2 * k + 1)) for k in range(n_chip)])

    def col_send(l, h, name, value):
        buf = halves[h][name]
        buf[l, col] = value.astype(BF16)
        for t in (2, 1, 3):
            remote(h, name, 0, buf.at[l, col], buf.at[l, col], "col", lax.rem(col + t, n_col)).start()

    def col_sum(l, h, name, bias):
        buf = halves[h][name]
        got(h, name, 0, buf.at[l, pl.ds(0, n_col - 1)], "col")
        total = buf[l, 0].astype(F32)
        for j in range(1, n_col):
            total = total + buf[l, j].astype(F32)
        rows = slice(h * part, (h + 1) * part)
        state[rows] = (state[rows].astype(F32) + (total + bias)).astype(BF16)
        sent(h, name, 0, buf.at[l, pl.ds(0, n_col - 1)], "col")

    def project(l, h):
        b = halves[h]
        y = local_norm(l, h, "st1", 0, g1, b1)
        if h == 0:
            big_copy(WQ, l).wait()
        res = jnp.dot(y, wq[l], preferred_element_type=F32).astype(BF16)
        for j in range(n_row):
            b["q_send"][l, j] = res[:, j * hd:(j + 1) * hd]
        for j in row_order + [partner]:
            remote(h, "q", 0, b["q_send"].at[l, j], b["q_recv"].at[l, row], "row", j).start()
        b["q_recv"][l, row] = b["q_send"][l, row]
        if h == 0:
            big_copy(WK, l).wait()
            big_copy(WV, l).wait()
        for w, (name, w_ref) in enumerate((("kd", wk), ("vd", wv))):
            res = jnp.dot(y, w_ref[l], preferred_element_type=F32)
            even = jnp.concatenate([res[:, 2 * k * hd:(2 * k + 1) * hd] for k in range(n_chip)], axis=1)
            odd = jnp.concatenate([res[:, (2 * k + 1) * hd:(2 * k + 2) * hd] for k in range(n_chip)], axis=1)
            b["kd_send"][l, w] = jnp.where(par == 0, odd, even).astype(BF16)
            remote(h, name, 0, b["kd_send"].at[l, w], b["kd_recv"].at[l, w], "row", partner).start()
            b["k_mine"][w] = jnp.where(par == 0, even, odd)

    def send_kv(l, h):
        b, first = halves[h], halves[0]
        got(h, "st1p", 0, b["st_recv"].at[l, 0, 0])
        merged = pair_merge(l, h, 0)
        for w, (d_name, name) in enumerate((("kd", "k"), ("vd", "v"))):
            got(h, d_name, 0, b["kd_recv"].at[l, w])
            own, other = b["k_mine"][w], b["kd_recv"][l, w].astype(F32)
            gb_own, gb_other = first["k_mine"][w, part:], first["kd_recv"][l, w, part:].astype(F32)
            both = merged(own, other, gb_own[0:1], gb_other[0:1])
            if h == 0:
                both = jnp.concatenate([both, gb_own + gb_other], axis=0)
            both = both.astype(BF16)
            for k in range(n_chip):
                b["k_send"][l, w, k] = both[:, k * hd:(k + 1) * hd]
            for off in offs[:-1]:
                k = chips[off]
                remote(h, name, 0, b["k_send"].at[l, w, k], b["k_recv"].at[l, w, chip], "row", 2 * k + par).start()
            b["k_recv"][l, w, chip] = b["k_send"][l, w, chip]

    def collect(parts, firsts, coefs, bias, l):
        total = pick_slice(bias, l, row * hd, hd)
        for value, first, (scale, shift) in zip(parts, firsts, coefs):
            gb = first.astype(F32)
            total = total + (scale * value[:part].astype(F32) + (shift * gb[0:1] + gb[1:2]))
        return total

    def attend(l, h):
        b, first = halves[h], halves[0]
        base = h * part
        got(h, "st1", 0, b["st_recv"].at[l, 0, pl.ds(0, n_row - 2)])
        coef = global_norm([stats(l, h, 0, j) for j in range(n_row)])
        coef_pair = pair_coefficients(l, h, 0)
        got(h, "q", 0, b["q_recv"].at[l, pl.ds(0, n_row - 1)])
        q = collect([b["q_recv"][l, j] for j in range(n_row)], [first["q_recv"][l, j, part:] for j in range(n_row)],
                    coef, bq, l)
        q = (q * (hd ** -0.5)).astype(BF16).astype(F32)
        group = 16
        rowi = lax.broadcasted_iota(jnp.int32, (group, 1), 0)
        if h == 0:
            big_copy(KC, l).wait()
        parts = []
        for g in range(part // group):
            q_g = q[g * group:(g + 1) * group]
            lhs = jnp.concatenate([jnp.where(rowi == i, q_g, 0.0) for i in range(group)], axis=1).astype(BF16)
            k_g = jnp.concatenate([kc[l, base + g * group + i] for i in range(group)], axis=1)
            parts.append(lax.dot_general(lhs, k_g, (((1,), (1,)), ((), ())), preferred_element_type=F32))
        scores = jnp.concatenate(parts, axis=0)
        spread = lax.broadcasted_iota(jnp.int32, (part, batch), 0) + base
        spread = spread == lax.broadcasted_iota(jnp.int32, (part, batch), 1)
        lens = jnp.sum(jnp.where(spread, len_v[...], 0), axis=1, keepdims=True)
        scores = jnp.where(lax.broadcasted_iota(jnp.int32, (part, keys), 1) < lens, scores, -jnp.inf)

        def fresh(w, name, bias):
            got(h, name, 0, b["k_recv"].at[l, w, pl.ds(0, n_chip - 1)])
            return collect([b["k_recv"][l, w, k] for k in range(n_chip)],
                           [first["k_recv"][l, w, k, part:] for k in range(n_chip)], coef_pair, bias, l).astype(BF16)

        k_new = fresh(0, "k", bk)
        s_new = jnp.sum(q * k_new.astype(F32), axis=1, keepdims=True)
        peak = jnp.maximum(jnp.max(scores, axis=1, keepdims=True), s_new)
        e = jnp.exp(scores - peak)
        e_new = jnp.exp(s_new - peak)
        mass = jnp.sum(e, axis=1, keepdims=True) + e_new
        prob = (e / mass).astype(BF16).astype(F32)
        prob_new = (e_new / mass).astype(BF16).astype(F32)
        if h == 0:
            big_copy(VC, l).wait()
        outs = []
        for g in range(part // group):
            p_g = prob[g * group:(g + 1) * group]
            lhs = jnp.concatenate([jnp.where(rowi // 2 == i, p_g, 0.0) for i in range(group // 2)],
                                  axis=1).astype(BF16)
            at = base + g * group
            v_g = jnp.concatenate([jnp.concatenate([vc[l, at + 2 * i], vc[l, at + 2 * i + 1]], axis=1)
                                   for i in range(group // 2)], axis=0)
            out = jnp.dot(lhs, v_g, preferred_element_type=F32)
            outs.append(jnp.where(rowi % 2 == 0, out[:, :hd], out[:, hd:]))
        v_new = fresh(1, "v", bv)
        mixed = jnp.concatenate(outs, axis=0) + prob_new * v_new.astype(F32)
        b["ag"][l, row] = mixed.astype(BF16)
        for j in row_order + [partner]:
            remote(h, "ag", 0, b["ag"].at[l, row], b["ag"].at[l, row], "row", j).start()
        b["kv_stage"][l, 0] = k_new
        b["kv_stage"][l, 1] = v_new
        kv_copy(l, h, 0).start()
        kv_copy(l, h, 1).start()

    def kv_copy(l, h, w):
        return pltpu.make_async_copy(halves[h]["kv_stage"].at[l, w], (k_out, v_out)[w].at[l, pl.ds(h * part, part)],
                                     out_sem.at[l, h, w])

    def out_product(l, h):
        ag = halves[h]["ag"]
        if h == 0:
            big_copy(WO, l).wait()
        got(h, "ag", 0, ag.at[l, pl.ds(0, n_row - 1)])
        gathered = jnp.concatenate([ag[l, j] for j in range(n_row)], axis=1)
        col_send(l, h, "wo", jnp.dot(gathered, wo[l], preferred_element_type=F32))

    def up(l, h):
        b, first = halves[h], halves[0]
        col_sum(l, h, "wo", pick(bo, l))
        y2 = local_norm(l, h, "st2", 1, g2, b2)
        if h == 0:
            big_copy(W1, l).wait()

        def block(j):
            return jnp.dot(y2, w1[l, :, pl.ds(pl.multiple_of(j * ffb, ffb), ffb)], preferred_element_type=F32)

        for some in (offs[:2], offs[2:]):
            blocks = [block(2 * chips[off] + 1 - par).astype(BF16) for off in some]
            for off, value in zip(some, blocks):
                b["fd_send"][l, chips[off]] = value
            for off in some:
                k = chips[off]
                remote(h, "fd", k, b["fd_send"].at[l, k], b["fd_recv"].at[l, k], "row", partner).start()
        blocks = [block(2 * chips[off] + par) for off in offs]
        for off, value in zip(offs, blocks):
            b["f_mine"][chips[off]] = value
        got(h, "st2p", 0, b["st_recv"].at[l, 1, 0])
        merged = pair_merge(l, h, 1)
        for off in offs:
            k = chips[off]
            got(h, "fd", k, b["fd_recv"].at[l, k])
            gb_own, gb_other = first["f_mine"][k, part:], first["fd_recv"][l, k, part:].astype(F32)
            both = merged(b["f_mine"][k], b["fd_recv"][l, k].astype(F32), gb_own[0:1], gb_other[0:1]).astype(BF16)
            if h == 0:
                gb = gb_own + gb_other
                gb = jnp.concatenate([gb[0:1], gb[1:2]], axis=1)
                tile = jnp.concatenate([gb[:, i * 128:(i + 1) * 128] for i in range(2 * lanes)], axis=0)
            if off:
                b["fi_send"][l, k] = both
                remote(h, "fi", 0, b["fi_send"].at[l, k], b["fi_recv"].at[l, chip], "row", 2 * k + par).start()
                if h == 0:
                    b["fg_send"][l, k] = tile
                    remote(h, "fg", 0, b["fg_send"].at[l, k], b["fg_recv"].at[l, chip], "row", 2 * k + par).start()
            else:
                b["fi_recv"][l, k] = both
                if h == 0:
                    b["fg_recv"][l, k] = tile

    def activate(l, h):
        b, first = halves[h], halves[0]
        ug = b["ug"]
        got(h, "st2", 0, b["st_recv"].at[l, 1, pl.ds(0, n_row - 2)])
        coef = pair_coefficients(l, h, 1)
        total = pick_slice(bf1, l, row * ffb, ffb)
        if h == 0:
            got(h, "fg", 0, b["fg_recv"].at[l, pl.ds(0, n_chip - 1)])
        got(h, "fi", 0, b["fi_recv"].at[l, pl.ds(0, n_chip - 1)])
        for k in range(n_chip):
            tile = first["fg_recv"][l, k]
            g = jnp.concatenate([tile[i:i + 1] for i in range(lanes)], axis=1)
            shift = jnp.concatenate([tile[lanes + i:lanes + i + 1] for i in range(lanes)], axis=1)
            total = total + (coef[k][0] * b["fi_recv"][l, k].astype(F32) + (coef[k][1] * g + shift))
        ug[l, row] = jnp.maximum(total.astype(BF16), 0)
        for off in offs[:-1]:
            remote(h, "ug", n_chip - off, ug.at[l, row], ug.at[l, row], "row", 2 * chips[off] + par).start()
        remote(h, "ug", 0, ug.at[l, row], ug.at[l, row], "row", partner).start()

    def same(off):
        return 2 * chips[off] + par

    def cross(off):
        return 2 * chips[off] + 1 - par

    def fc2_block(l, h, j):
        return jnp.dot(halves[h]["ug"][l, j], w2[l, pl.ds(pl.multiple_of(j * ffb, ffb), ffb), :],
                       preferred_element_type=F32)

    def pass_on(l, h, off):
        ug = halves[h]["ug"]
        got(h, "ug", off, ug.at[l, same(off)])
        remote(h, "ug", n_chip - 1 + off, ug.at[l, same(off)], ug.at[l, same(off)], "row", partner).start()

    def down_first(l, h):
        if h == 0:
            big_copy(W2, l).wait()
        got(h, "ug", 0, halves[h]["ug"].at[l, partner])
        halves[h]["acc"][...] = fc2_block(l, h, row) + fc2_block(l, h, partner)

    def down_near(l, h):
        pass_on(l, h, 1)
        pass_on(l, h, 3)
        acc = halves[h]["acc"]
        acc[...] = acc[...] + (fc2_block(l, h, same(1)) + fc2_block(l, h, same(3)))

    def down_far(l, h):
        ug, acc = halves[h]["ug"], halves[h]["acc"]
        pass_on(l, h, 2)
        got(h, "ug", n_chip, ug.at[l, cross(1)])
        got(h, "ug", n_chip + 2, ug.at[l, cross(3)])
        acc[...] = acc[...] + (fc2_block(l, h, same(2)) + fc2_block(l, h, cross(1)) + fc2_block(l, h, cross(3)))

    def down_last(l, h):
        got(h, "ug", n_chip + 1, halves[h]["ug"].at[l, cross(2)])
        col_send(l, h, "fo", halves[h]["acc"][...] + fc2_block(l, h, cross(2)))

    def drain(l, h):
        b = halves[h]
        for which, name in ((0, "st1"), (1, "st2")):
            sent(h, name, 0, b["st_recv"].at[l, which, pl.ds(0, n_row - 2)])
            sent(h, name + "p", 0, b["st_recv"].at[l, which, 0])
        sent(h, "q", 0, b["q_recv"].at[l, pl.ds(0, n_row - 1)])
        for w, (d, i) in enumerate((("kd", "k"), ("vd", "v"))):
            sent(h, d, 0, b["kd_send"].at[l, w])
            sent(h, i, 0, b["k_send"].at[l, w, pl.ds(0, n_chip - 1)])
        sent(h, "ag", 0, b["ag"].at[l, pl.ds(0, n_row - 1)])
        for k in range(n_chip):
            sent(h, "fd", k, b["fd_send"].at[l, k])
        sent(h, "fi", 0, b["fi_send"].at[l, pl.ds(0, n_chip - 1)])
        if h == 0:
            sent(h, "fg", 0, b["fg_send"].at[l, pl.ds(0, n_chip - 1)])
        for j in range(n_row - 1):
            sent(h, "ug", j, b["ug"].at[l, j])

    def layer(l, carry):
        for h in range(HALVES):
            pl.when(l > 0)(functools.partial(finish_layer, l - 1, h))
            project(l, h)
        pl.when(l == 0)(rest_of_bulk)
        for stage in (send_kv, attend, out_product, up, activate):
            for h in range(HALVES):
                stage(l, h)
        down_first(l, 0)
        down_first(l, 1)
        down_near(l, 0)
        down_far(l, 0)
        down_near(l, 1)
        down_last(l, 0)
        down_far(l, 1)
        down_last(l, 1)
        for h in range(HALVES):
            drain(l, h)
        return carry

    def finish_layer(l, h):
        col_sum(jnp.maximum(l, 0), h, "fo", pick(bf2, l))

    lax.fori_loop(0, n_layer, layer, 0)
    out_copies = [pltpu.make_async_copy(state.at[pl.ds(h * part, part)], h_out.at[pl.ds(h * part, part)],
                                        out_sem.at[0, h, 2]) for h in range(HALVES)]
    for h in range(HALVES):
        finish_layer(n_layer - 1, h)
        out_copies[h].start()
    for l in range(n_layer):
        for h in range(HALVES):
            kv_copy(l, h, 0).wait()
            kv_copy(l, h, 1).wait()
    for c in out_copies:
        c.wait()


def finish(h, k, v, h_out, k_out, v_out, h_v, k_v, v_v, sem_in, sem_out):
    loads = [pltpu.make_async_copy(s, d, sem_in.at[i]) for i, (s, d) in enumerate(((h, h_v), (k, k_v), (v, v_v)))]
    stores = [pltpu.make_async_copy(s, d, sem_out.at[i])
              for i, (s, d) in enumerate(((h_v, h_out), (k_v, k_out), (v_v, v_out)))]
    for c in loads:
        c.start()
    for c, d in zip(loads, stores):
        c.wait()
        d.start()
    for d in stores:
        d.wait()


def solution(mesh):
    n_row, n_col = mesh.shape["row"], mesh.shape["col"]
    n_chip = n_row // 2
    act_spec = P("dp", "row")
    cache_spec = P(None, "dp", ("col", "row"), None, None)
    fresh_spec = P(None, "dp", ("col", "row"), None)
    in_weight = P(None, "row", "col")
    out_weight = P(None, "col", "row")
    col_vec = P(None, "col")
    row_vec = P(None, "row")
    in_specs = (act_spec, P("dp"), cache_spec, cache_spec, row_vec, row_vec,
                in_weight, col_vec, in_weight, col_vec, in_weight, col_vec,
                out_weight, row_vec, row_vec, row_vec, in_weight, col_vec, out_weight, row_vec)

    def local_step(hidden, cache_len, k_cache, v_cache, ln1_g, ln1_b, w_q, b_q, w_k, b_k, w_v, b_v,
                   w_o, b_o, ln2_g, ln2_b, w_fc1, b_fc1, w_fc2, b_fc2):
        batch, width = hidden.shape
        n_layer, _, _, keys, hd = k_cache.shape
        ff = w_fc1.shape[2]
        ffb = ff // n_row
        table, n_sem = layout(n_chip)
        part = batch // HALVES
        args = (hidden, cache_len.reshape(1, batch), k_cache, v_cache, ln1_g, ln1_b, w_q, b_q, w_k, b_k, w_v, b_v,
                w_o, b_o, ln2_g, ln2_b, w_fc1, b_fc1, w_fc2, b_fc2)

        def vm(shape, dtype=BF16):
            return pltpu.VMEM(shape, dtype)

        local = [vm(a.shape, a.dtype) for a in args]
        local[2] = local[3] = vm((n_layer, batch, keys, hd))

        def half(h):
            rows = part + 16 if h == 0 else part
            gb = (n_layer, n_chip, 2 * ffb // 128, 128)
            shapes = dict(
                q_send=vm((n_layer, n_row, rows, hd)), q_recv=vm((n_layer, n_row, rows, hd)),
                kd_send=vm((n_layer, 2, rows, n_chip * hd)), kd_recv=vm((n_layer, 2, rows, n_chip * hd)),
                k_mine=vm((2, rows, n_chip * hd), F32),
                k_send=vm((n_layer, 2, n_chip, rows, hd)), k_recv=vm((n_layer, 2, n_chip, rows, hd)),
                kv_stage=vm((n_layer, 2, part, hd)), ag=vm((n_layer, n_row, part, hd)),
                st_send=vm((n_layer, 2, 8, 128), F32), st_recv=vm((n_layer, 2, n_row, 8, 128), F32),
                wo=vm((n_layer, n_col, part, width)), fo=vm((n_layer, n_col, part, width)),
                fd_send=vm((n_layer, n_chip, rows, ffb)), fd_recv=vm((n_layer, n_chip, rows, ffb)),
                f_mine=vm((n_chip, rows, ffb), F32),
                fi_send=vm((n_layer, n_chip, part, ffb)), fi_recv=vm((n_layer, n_chip, part, ffb)),
                ug=vm((n_layer, n_row, part, ffb)), acc=vm((part, width), F32))
            if h == 0:
                shapes.update(fg_send=vm(gb, F32), fg_recv=vm(gb, F32))
            return shapes

        dma = pltpu.SemaphoreType.DMA
        scratch = [local, [half(h) for h in range(HALVES)], vm((batch, width)),
                   [dma((12,)), dma((n_layer, 8)), dma((n_layer, HALVES, 3)), dma((n_sem,)), dma((n_sem,))]]
        out_shape = (jax.ShapeDtypeStruct((batch, width), BF16),
                     jax.ShapeDtypeStruct((n_layer, batch, hd), BF16),
                     jax.ShapeDtypeStruct((n_layer, batch, hd), BF16))
        h_out, k_new, v_new = pl.pallas_call(
            functools.partial(kernel, (n_layer, n_row, n_col, table)),
            out_shape=out_shape,
            in_specs=[pl.BlockSpec(memory_space=pl.ANY)] * len(args),
            out_specs=[pl.BlockSpec(memory_space=pl.ANY)] * 3,
            scratch_shapes=scratch,
            compiler_params=pltpu.CompilerParams(collective_id=0, has_side_effects=True,
                                                 vmem_limit_bytes=VLIM),
        )(*args)
        h_out, k_new, v_new = pl.pallas_call(
            finish, out_shape=out_shape,
            in_specs=[pl.BlockSpec(memory_space=pl.ANY)] * 3, out_specs=[pl.BlockSpec(memory_space=pl.ANY)] * 3,
            scratch_shapes=[vm(o.shape) for o in out_shape] + [pltpu.SemaphoreType.DMA((3,))] * 2,
        )(h_out, k_new, v_new)
        return h_out, k_new[:, :, None, :], v_new[:, :, None, :]

    return jax.shard_map(local_step, mesh=mesh, in_specs=in_specs,
                         out_specs=(act_spec, fresh_spec, fresh_spec), check_vma=False)
```

time: 82.2 us -> 75.4 us (0.917)
  Pallas kernels: 81.4 us -> 74.6 us
    pallas_call x1, Pallas kernels: 79.9 us -> 73 us  [local_step(): pl.pallas_call(functools.partial(kernel, (n_layer, n_row, n_col, table)),...]
where the time goes in v5:
time: 75.4 us; the launch traced here: 75.2 us
  Pallas kernels  74.6 us (99%)
    pallas_call x1, Pallas kernels, local_step(): pl.pallas_call(functools.partial(kernel, (n_layer, n_row, n_col, table)),...  73 us
    pallas_call x1, Pallas kernels, local_step(): pl.pallas_call(finish, out_shape=out_shape, in_specs=[pl.BlockSpec(memory...  1.54 us

profile of v5, /device:TPU:97, one launch (start us, length us, event | category | flops | bytes accessed | tf_op | source)
XLA Modules:
  0.0 75.2 jit_solution(9001913655576111830)
XLA Ops:
  0.6 73.0 %shard_map.211 = (bf16[64,512]{1,0:T(8,128)(2,1)}, bf16[2,64,128]{2,1,0:T(8,128)(2,1)}, bf16[2,64,128]{2,1,0:T(8,128)(2,1)}) custom-call(bf16[64,512]{1,0:T(8,128)(2,1)} %hid_hbm.1, s32[1,64]{1,0:T(1,128)} %bitcast.7, bf16[2,64,1,256,128]{4,3,2,1,0:T(8,128)(2,1)} %kc_hbm.1, bf16[2,64,1,256,128]{4,3,2,1,0:T(8,128)(2,1)} %vc_hbm.1, bf16[2,512]{1,0:T(2,128)(2,1)} %g1_hbm.1, ...), custom_call_target="tpu_custom_call" | custom-call | tf_op jit(solution)/shard_map/pallas_call | solution.py:554
  73.7 1.5 %shard_map.212 = (bf16[64,512]{1,0:T(8,128)(2,1)}, bf16[2,64,128]{2,1,0:T(8,128)(2,1)}, bf16[2,64,128]{2,1,0:T(8,128)(2,1)}) custom-call(bf16[64,512]{1,0:T(8,128)(2,1)} %get-tuple-element.9.h, bf16[2,64,128]{2,1,0:T(8,128)(2,1)} %get-tuple-element.10.k, bf16[2,64,128]{2,1,0:T(8,128)(2,1)} %get-tuple-element.11.v), custom_call_target="tpu_custom_call" | custom-call | tf_op jit(solution)/shard_map/pallas_call | solution.py:563

commit v6 on v5

--- a/solution.py
+++ b/solution.py
@@ -8,7 +8,7 @@
 from jax.sharding import PartitionSpec as P
 
 EPS_LN = 1e-5
-VLIM = 66 * 1000 * 1000
+VLIM = 64 * 1000 * 1000
 MESH = pl.DeviceIdType.MESH
 F32 = jnp.float32
 BF16 = jnp.bfloat16
@@ -27,12 +27,17 @@
 HALVES = 2
 
 
-def layout(n_chip):
-    sems = Sems()
-    names = dict(st1=1, st1p=1, st2=1, st2p=1, q=1, kd=1, vd=1, k=1, v=1, ag=1, wo=1, fd=n_chip, fi=1, fg=1,
-                 ug=2 * n_chip - 1, fo=1)
-    table = [{name: sems.take(n) for name, n in names.items()} for _ in range(HALVES)]
-    return table, sems.count
+def layout():
+    recv = dict(st1=1, st1p=1, st2=1, st2p=1, q=1, kd=1, vd=1, k=1, v=1, ag=1, wo=1, fd=2, fi=1, fg=1, ug=5, fo=1)
+    send = dict(st1=1, st2=1, q=1, kd=1, k=1, ag=1, wo=1, fd=1, fi=1, fg=1, ug=1, fo=1)
+    tables = []
+    for names in (send, recv):
+        sems = Sems()
+        tables.append(([{name: sems.take(n) for name, n in names.items()} for _ in range(HALVES)], sems))
+    return [t for t, _ in tables], [c.count for _, c in tables]
+
+
+SENT_WITH = dict(st1p="st1", st2p="st2", vd="kd", v="k")
 
 
 def kernel(dims, hid_hbm, len_hbm, kc_hbm, vc_hbm, g1_hbm, b1_hbm, wq_hbm, bq_hbm, wk_hbm, bk_hbm, wv_hbm, bv_hbm,
@@ -40,7 +45,7 @@
            h_out, k_out, v_out, local, halves, state, sem):
     n_layer, n_row, n_col, table = dims
     hid_v, len_v, kc, vc, g1, b1, wq, bq, wk, bk, wv, bv, wo, bo, g2, b2, w1, bf1, w2, bf2 = local
-    small_sem, big_sem, out_sem, ssem, rsem = sem
+    small_sem, big_sem, ssem, rsem = sem
     n_chip = n_row // 2
     row = lax.axis_index("row")
     col = lax.axis_index("col")
@@ -77,21 +82,26 @@
         src = s.at[l, :, 0] if i in (KC, VC) else s.at[l]
         return pltpu.make_async_copy(src, d.at[l], big_sem.at[l, i])
 
-    for c in small_copies:
+    for c in small_copies[:3]:
         c.start()
     for i in (WQ, WK, WV):
         big_copy(i, 0).start()
+    for c in small_copies[3:]:
+        c.start()
     small_copies[0].wait()
     state[...] = hid_v[...]
 
+
     def enter():
         pl.semaphore_wait(barrier, n_row - 1 + n_col - 1)
 
-    def rest_of_small():
-        for c in small_copies[1:]:
+    def norm_vectors():
+        for c in small_copies[1:3]:
             c.wait()
 
-    def rest_of_bulk():
+    def rest_of_loads():
+        for c in small_copies[3:]:
+            c.wait()
         for i in (KC, VC, WO, W1, W2):
             big_copy(i, 0).start()
         for l in range(1, n_layer):
@@ -99,9 +109,9 @@
                 big_copy(i, l).start()
 
     def remote(h, name, i, src, dst, axis, target):
-        at = table[h][name] + i
-        return pltpu.make_async_remote_copy(src_ref=src, dst_ref=dst, send_sem=ssem.at[at], recv_sem=rsem.at[at],
-                                            device_id={axis: target}, device_id_type=MESH)
+        return pltpu.make_async_remote_copy(
+            src_ref=src, dst_ref=dst, send_sem=ssem.at[table[0][h][SENT_WITH.get(name, name)]],
+            recv_sem=rsem.at[table[1][h][name] + i], device_id={axis: target}, device_id_type=MESH)
 
     def same_bytes(h, name, i, ref, axis):
         return remote(h, name, i, ref, ref, axis, partner if axis == "row" else lax.rem(col + 1, n_col))
@@ -109,8 +119,8 @@
     def got(h, name, i, ref, axis="row"):
         same_bytes(h, name, i, ref, axis).wait_recv()
 
-    def sent(h, name, i, ref, axis="row"):
-        same_bytes(h, name, i, ref, axis).wait_send()
+    def sent(h, name, ref, axis="row"):
+        same_bytes(h, name, 0, ref, axis).wait_send()
 
     def pick(ref, l):
         rows = ref[...].astype(F32)
@@ -134,7 +144,7 @@
     def to_column(line):
         return jnp.sum(jnp.where(eye, line, 0.0), axis=1, keepdims=True)
 
-    def local_norm(l, h, name, which, gain, shift):
+    def local_norm(l, h, name, which, gain, shift, entering=False):
         st_send, st_recv = halves[h]["st_send"], halves[h]["st_recv"]
         x = state[h * part:(h + 1) * part].astype(F32)
         c = jnp.sum(x, axis=1, keepdims=True) / width
@@ -143,21 +153,24 @@
         sub = lax.broadcasted_iota(jnp.int32, (8, 128), 0)
         tile = jnp.where(sub == 0, to_row(c), jnp.where(sub == 1, to_row(v), 0.0))
         st_send[l, which] = tile
-        if which == 0 and h == 0:
-            pl.when(l == 0)(enter)
-        for j in row_order:
-            remote(h, name, 0, st_send.at[l, which], st_recv.at[l, which, row], "row", j).start()
-        remote(h, name + "p", 0, st_send.at[l, which], st_recv.at[l, which, row], "row", partner).start()
         st_recv[l, which, row] = tile
-        if which == 0 and h == 0:
-            pl.when(l == 0)(rest_of_small)
+
+        def send():
+            for j in row_order:
+                remote(h, name, 0, st_send.at[l, which], st_recv.at[l, which, row], "row", j).start()
+            remote(h, name + "p", 0, st_send.at[l, which], st_recv.at[l, which, row], "row", partner).start()
+
+        if entering:
+            norm_vectors()
+        else:
+            send()
         g, b = pick(gain, l), pick(shift, l)
         y = (xc * lax.rsqrt(v + EPS_LN) * g).astype(BF16)
         if h:
-            return y
+            return y, send
         extra = lax.broadcasted_iota(jnp.int32, (16, 1), 0)
         extra = jnp.where(extra == 0, g, jnp.where(extra == 1, b, 0.0))
-        return jnp.concatenate([y, extra.astype(BF16)], axis=0)
+        return jnp.concatenate([y, extra.astype(BF16)], axis=0), send
 
     def scale_of(v):
         return (v + EPS_LN) * lax.rsqrt(v + EPS_LN)
@@ -205,19 +218,30 @@
             total = total + buf[l, j].astype(F32)
         rows = slice(h * part, (h + 1) * part)
         state[rows] = (state[rows].astype(F32) + (total + bias)).astype(BF16)
-        sent(h, name, 0, buf.at[l, pl.ds(0, n_col - 1)], "col")
-
-    def project(l, h):
+        sent(h, name, buf.at[l, pl.ds(0, n_col - 1)], "col")
+
+    def project_q(l, h, entering=False):
         b = halves[h]
-        y = local_norm(l, h, "st1", 0, g1, b1)
+        y, send_stats = local_norm(l, h, "st1", 0, g1, b1, entering)
         if h == 0:
             big_copy(WQ, l).wait()
         res = jnp.dot(y, wq[l], preferred_element_type=F32).astype(BF16)
         for j in range(n_row):
             b["q_send"][l, j] = res[:, j * hd:(j + 1) * hd]
+        b["y"][...] = y
+        if entering:
+            enter()
+            send_stats()
+
+    def send_q(l, h):
+        b = halves[h]
         for j in row_order + [partner]:
             remote(h, "q", 0, b["q_send"].at[l, j], b["q_recv"].at[l, row], "row", j).start()
         b["q_recv"][l, row] = b["q_send"][l, row]
+
+    def project_kv(l, h):
+        b = halves[h]
+        y = b["y"][...]
         if h == 0:
             big_copy(WK, l).wait()
             big_copy(WV, l).wait()
@@ -311,14 +335,8 @@
         b["ag"][l, row] = mixed.astype(BF16)
         for j in row_order + [partner]:
             remote(h, "ag", 0, b["ag"].at[l, row], b["ag"].at[l, row], "row", j).start()
-        b["kv_stage"][l, 0] = k_new
-        b["kv_stage"][l, 1] = v_new
-        kv_copy(l, h, 0).start()
-        kv_copy(l, h, 1).start()
-
-    def kv_copy(l, h, w):
-        return pltpu.make_async_copy(halves[h]["kv_stage"].at[l, w], (k_out, v_out)[w].at[l, pl.ds(h * part, part)],
-                                     out_sem.at[l, h, w])
+        k_out[l, base:base + part] = k_new
+        v_out[l, base:base + part] = v_new
 
     def out_product(l, h):
         ag = halves[h]["ag"]
@@ -331,7 +349,7 @@
     def up(l, h):
         b, first = halves[h], halves[0]
         col_sum(l, h, "wo", pick(bo, l))
-        y2 = local_norm(l, h, "st2", 1, g2, b2)
+        y2, _ = local_norm(l, h, "st2", 1, g2, b2)
         if h == 0:
             big_copy(W1, l).wait()
 
@@ -344,7 +362,8 @@
                 b["fd_send"][l, chips[off]] = value
             for off in some:
                 k = chips[off]
-                remote(h, "fd", k, b["fd_send"].at[l, k], b["fd_recv"].at[l, k], "row", partner).start()
+                remote(h, "fd", offs.index(off) // 2, b["fd_send"].at[l, k], b["fd_recv"].at[l, k], "row",
+                       partner).start()
         blocks = [block(2 * chips[off] + par) for off in offs]
         for off, value in zip(offs, blocks):
             b["f_mine"][chips[off]] = value
@@ -352,7 +371,8 @@
         merged = pair_merge(l, h, 1)
         for off in offs:
             k = chips[off]
-            got(h, "fd", k, b["fd_recv"].at[l, k])
+            if off in (offs[0], offs[2]):
+                got(h, "fd", offs.index(off) // 2, b["fd_recv"].at[l, pl.ds(0, 2)])
             gb_own, gb_other = first["f_mine"][k, part:], first["fd_recv"][l, k, part:].astype(F32)
             both = merged(b["f_mine"][k], b["fd_recv"][l, k].astype(F32), gb_own[0:1], gb_other[0:1]).astype(BF16)
             if h == 0:
@@ -386,7 +406,7 @@
             total = total + (coef[k][0] * b["fi_recv"][l, k].astype(F32) + (coef[k][1] * g + shift))
         ug[l, row] = jnp.maximum(total.astype(BF16), 0)
         for off in offs[:-1]:
-            remote(h, "ug", n_chip - off, ug.at[l, row], ug.at[l, row], "row", 2 * chips[off] + par).start()
+            remote(h, "ug", 2 - off % 2, ug.at[l, row], ug.at[l, row], "row", 2 * chips[off] + par).start()
         remote(h, "ug", 0, ug.at[l, row], ug.at[l, row], "row", partner).start()
 
     def same(off):
@@ -401,8 +421,7 @@
 
     def pass_on(l, h, off):
         ug = halves[h]["ug"]
-        got(h, "ug", off, ug.at[l, same(off)])
-        remote(h, "ug", n_chip - 1 + off, ug.at[l, same(off)], ug.at[l, same(off)], "row", partner).start()
+        remote(h, "ug", 4 - off % 2, ug.at[l, same(off)], ug.at[l, same(off)], "row", partner).start()
 
     def down_first(l, h):
         if h == 0:
@@ -411,6 +430,7 @@
         halves[h]["acc"][...] = fc2_block(l, h, row) + fc2_block(l, h, partner)
 
     def down_near(l, h):
+        got(h, "ug", 1, halves[h]["ug"].at[l, pl.ds(0, 2)])
         pass_on(l, h, 1)
         pass_on(l, h, 3)
         acc = halves[h]["acc"]
@@ -418,47 +438,51 @@
 
     def down_far(l, h):
         ug, acc = halves[h]["ug"], halves[h]["acc"]
+        got(h, "ug", 2, ug.at[l, same(2)])
         pass_on(l, h, 2)
-        got(h, "ug", n_chip, ug.at[l, cross(1)])
-        got(h, "ug", n_chip + 2, ug.at[l, cross(3)])
+        got(h, "ug", 3, ug.at[l, pl.ds(0, 2)])
         acc[...] = acc[...] + (fc2_block(l, h, same(2)) + fc2_block(l, h, cross(1)) + fc2_block(l, h, cross(3)))
 
     def down_last(l, h):
-        got(h, "ug", n_chip + 1, halves[h]["ug"].at[l, cross(2)])
+        got(h, "ug", 4, halves[h]["ug"].at[l, cross(2)])
         col_send(l, h, "fo", halves[h]["acc"][...] + fc2_block(l, h, cross(2)))
 
     def drain(l, h):
         b = halves[h]
         for which, name in ((0, "st1"), (1, "st2")):
-            sent(h, name, 0, b["st_recv"].at[l, which, pl.ds(0, n_row - 2)])
-            sent(h, name + "p", 0, b["st_recv"].at[l, which, 0])
-        sent(h, "q", 0, b["q_recv"].at[l, pl.ds(0, n_row - 1)])
-        for w, (d, i) in enumerate((("kd", "k"), ("vd", "v"))):
-            sent(h, d, 0, b["kd_send"].at[l, w])
-            sent(h, i, 0, b["k_send"].at[l, w, pl.ds(0, n_chip - 1)])
-        sent(h, "ag", 0, b["ag"].at[l, pl.ds(0, n_row - 1)])
-        for k in range(n_chip):
-            sent(h, "fd", k, b["fd_send"].at[l, k])
-        sent(h, "fi", 0, b["fi_send"].at[l, pl.ds(0, n_chip - 1)])
-        if h == 0:
-            sent(h, "fg", 0, b["fg_send"].at[l, pl.ds(0, n_chip - 1)])
-        for j in range(n_row - 1):
-            sent(h, "ug", j, b["ug"].at[l, j])
+            sent(h, name, b["st_recv"].at[l, which, pl.ds(0, n_row - 1)])
+        sent(h, "q", b["q_recv"].at[l, pl.ds(0, n_row - 1)])
+        sent(h, "kd", b["kd_send"].at[l])
+        sent(h, "k", b["k_send"].at[l, :, pl.ds(0, n_chip - 1)])
+        sent(h, "ag", b["ag"].at[l, pl.ds(0, n_row - 1)])
+        sent(h, "fd", b["fd_send"].at[l])
+        sent(h, "fi", b["fi_send"].at[l, pl.ds(0, n_chip - 1)])
+        if h == 0:
+            sent(h, "fg", b["fg_send"].at[l, pl.ds(0, n_chip - 1)])
+        sent(h, "ug", b["ug"].at[l, pl.ds(0, n_row - 1)])
 
     def layer(l, carry):
-        for h in range(HALVES):
-            pl.when(l > 0)(functools.partial(finish_layer, l - 1, h))
-            project(l, h)
-        pl.when(l == 0)(rest_of_bulk)
-        for stage in (send_kv, attend, out_product, up, activate):
+        def later():
+            finish_layer(l - 1, 0)
+            project_q(l, 0)
+
+        pl.when(l > 0)(later)
+        send_q(l, 0)
+        project_kv(l, 0)
+        pl.when(l > 0)(functools.partial(finish_layer, l - 1, 1))
+        project_q(l, 1)
+        send_q(l, 1)
+        pl.when(l == 0)(rest_of_loads)
+        send_kv(l, 0)
+        project_kv(l, 1)
+        send_kv(l, 1)
+        for stage in (attend, out_product, up, activate, down_first):
             for h in range(HALVES):
                 stage(l, h)
-        down_first(l, 0)
-        down_first(l, 1)
         down_near(l, 0)
         down_far(l, 0)
+        down_last(l, 0)
         down_near(l, 1)
-        down_last(l, 0)
         down_far(l, 1)
         down_last(l, 1)
         for h in range(HALVES):
@@ -468,31 +492,19 @@
     def finish_layer(l, h):
         col_sum(jnp.maximum(l, 0), h, "fo", pick(bf2, l))
 
+    project_q(0, 0, entering=True)
     lax.fori_loop(0, n_layer, layer, 0)
-    out_copies = [pltpu.make_async_copy(state.at[pl.ds(h * part, part)], h_out.at[pl.ds(h * part, part)],
-                                        out_sem.at[0, h, 2]) for h in range(HALVES)]
     for h in range(HALVES):
         finish_layer(n_layer - 1, h)
-        out_copies[h].start()
-    for l in range(n_layer):
-        for h in range(HALVES):
-            kv_copy(l, h, 0).wait()
-            kv_copy(l, h, 1).wait()
-    for c in out_copies:
+    h_out[...] = state[...]
+
+
+def finish(h, k, v, h_out, k_out, v_out, sem):
+    copies = [pltpu.make_async_copy(s, d, sem.at[i]) for i, (s, d) in enumerate(((h, h_out), (k, k_out), (v, v_out)))]
+    for c in copies:
+        c.start()
+    for c in copies:
         c.wait()
-
-
-def finish(h, k, v, h_out, k_out, v_out, h_v, k_v, v_v, sem_in, sem_out):
-    loads = [pltpu.make_async_copy(s, d, sem_in.at[i]) for i, (s, d) in enumerate(((h, h_v), (k, k_v), (v, v_v)))]
-    stores = [pltpu.make_async_copy(s, d, sem_out.at[i])
-              for i, (s, d) in enumerate(((h_v, h_out), (k_v, k_out), (v_v, v_out)))]
-    for c in loads:
-        c.start()
-    for c, d in zip(loads, stores):
-        c.wait()
-        d.start()
-    for d in stores:
-        d.wait()
 
 
 def solution(mesh):
@@ -515,7 +527,7 @@
         n_layer, _, _, keys, hd = k_cache.shape
         ff = w_fc1.shape[2]
         ffb = ff // n_row
-        table, n_sem = layout(n_chip)
+        table, n_sem = layout()
         part = batch // HALVES
         args = (hidden, cache_len.reshape(1, batch), k_cache, v_cache, ln1_g, ln1_b, w_q, b_q, w_k, b_k, w_v, b_v,
                 w_o, b_o, ln2_g, ln2_b, w_fc1, b_fc1, w_fc2, b_fc2)
@@ -534,7 +546,7 @@
                 kd_send=vm((n_layer, 2, rows, n_chip * hd)), kd_recv=vm((n_layer, 2, rows, n_chip * hd)),
                 k_mine=vm((2, rows, n_chip * hd), F32),
                 k_send=vm((n_layer, 2, n_chip, rows, hd)), k_recv=vm((n_layer, 2, n_chip, rows, hd)),
-                kv_stage=vm((n_layer, 2, part, hd)), ag=vm((n_layer, n_row, part, hd)),
+                y=vm((rows, width)), ag=vm((n_layer, n_row, part, hd)),
                 st_send=vm((n_layer, 2, 8, 128), F32), st_recv=vm((n_layer, 2, n_row, 8, 128), F32),
                 wo=vm((n_layer, n_col, part, width)), fo=vm((n_layer, n_col, part, width)),
                 fd_send=vm((n_layer, n_chip, rows, ffb)), fd_recv=vm((n_layer, n_chip, rows, ffb)),
@@ -547,24 +559,23 @@
 
         dma = pltpu.SemaphoreType.DMA
         scratch = [local, [half(h) for h in range(HALVES)], vm((batch, width)),
-                   [dma((12,)), dma((n_layer, 8)), dma((n_layer, HALVES, 3)), dma((n_sem,)), dma((n_sem,))]]
+                   [dma((12,)), dma((n_layer, 8)), dma((n_sem[0],)), dma((n_sem[1],))]]
         out_shape = (jax.ShapeDtypeStruct((batch, width), BF16),
                      jax.ShapeDtypeStruct((n_layer, batch, hd), BF16),
                      jax.ShapeDtypeStruct((n_layer, batch, hd), BF16))
-        h_out, k_new, v_new = pl.pallas_call(
+        kept = pl.pallas_call(
             functools.partial(kernel, (n_layer, n_row, n_col, table)),
-            out_shape=out_shape,
+            out_shape=[pltpu.VMEM(o.shape, o.dtype) for o in out_shape],
             in_specs=[pl.BlockSpec(memory_space=pl.ANY)] * len(args),
-            out_specs=[pl.BlockSpec(memory_space=pl.ANY)] * 3,
+            out_specs=[pl.BlockSpec(memory_space=pltpu.VMEM)] * 3,
             scratch_shapes=scratch,
-            compiler_params=pltpu.CompilerParams(collective_id=0, has_side_effects=True,
-                                                 vmem_limit_bytes=VLIM),
+            compiler_params=pltpu.CompilerParams(collective_id=0, has_side_effects=True, vmem_limit_bytes=VLIM),
         )(*args)
         h_out, k_new, v_new = pl.pallas_call(
             finish, out_shape=out_shape,
-            in_specs=[pl.BlockSpec(memory_space=pl.ANY)] * 3, out_specs=[pl.BlockSpec(memory_space=pl.ANY)] * 3,
-            scratch_shapes=[vm(o.shape) for o in out_shape] + [pltpu.SemaphoreType.DMA((3,))] * 2,
-        )(h_out, k_new, v_new)
+            in_specs=[pl.BlockSpec(memory_space=pltpu.VMEM)] * 3, out_specs=[pl.BlockSpec(memory_space=pl.ANY)] * 3,
+            scratch_shapes=[pltpu.SemaphoreType.DMA((3,))],
+        )(*[pltpu.with_memory_space_constraint(o, pltpu.VMEM) for o in kept])
         return h_out, k_new[:, :, None, :], v_new[:, :, None, :]
 
     return jax.shard_map(local_step, mesh=mesh, in_specs=in_specs,

time: 75.4 us -> 71.5 us (0.948)
  Pallas kernels: 74.6 us -> 70.8 us
    pallas_call x1, Pallas kernels: 73 us -> 70.1 us  [local_step(): pl.pallas_call(functools.partial(kernel, (n_layer, n_row, n_col, table)),...]
    pallas_call x1, Pallas kernels: 1.54 us -> 0.68 us  [local_step(): pl.pallas_call(finish, out_shape=out_shape, in_specs=[pl.BlockSpec(memory...]
where the time goes in v6:
time: 71.5 us; the launch traced here: 71.4 us
  Pallas kernels  70.8 us (99%)
    pallas_call x1, Pallas kernels, local_step(): pl.pallas_call(functools.partial(kernel, (n_layer, n_row, n_col, table)),...  70.1 us

profile of v6, /device:TPU:97, one launch (start us, length us, event | category | flops | bytes accessed | tf_op | source)
XLA Modules:
  0.0 71.4 jit_solution(2049660106743427693)
XLA Ops:
  0.6 70.1 %shard_map.211 = (bf16[64,512]{1,0:T(8,128)(2,1)S(1)}, bf16[2,64,128]{2,1,0:T(8,128)(2,1)S(1)}, bf16[2,64,128]{2,1,0:T(8,128)(2,1)S(1)}) custom-call(bf16[64,512]{1,0:T(8,128)(2,1)} %hid_hbm.1, s32[1,64]{1,0:T(1,128)} %bitcast.7, bf16[2,64,1,256,128]{4,3,2,1,0:T(8,128)(2,1)} %kc_hbm.1, bf16[2,64,1,256,128]{4,3,2,1,0:T(8,128)(2,1)} %vc_hbm.1, ...), custom_call_target="tpu_custom_call" | custom-call | tf_op jit(solution)/shard_map/pallas_call | solution.py:566
  70.8 0.7 shard_map.212
